TPU v7x, 128 devices: a whole 4x4x4 slice. The times are simulated.
128 devices in a mesh: seq: 8 (over x_lo, z), tp: 8 (over y, core), roll: 2 (over x_hi).
Axes of the slice: x: 4 (x_hi: 2, x_lo: 2; x = x_hi * 2 + x_lo), y: 4, z: 4, core: 2. Of those that a mesh axis runs over, the one named last changes fastest.
Arguments:
- hidden: bfloat16 [8, 3584], P('roll'), may hold values from -6 to 6
- norm_gain: bfloat16 [3584], replicated, may hold values from 0.25 to 1.75
- qkv_bias: bfloat16 [3072], replicated, may hold values from -20 to 20
- qkv_weight: bfloat16 [3584, 3072], P(('seq', 'tp', 'roll')), may hold values from -0.09375 to 0.09375
- out_weight: bfloat16 [3584, 2048], P(('seq', 'tp', 'roll')), may hold values from -0.125 to 0.125
- key_cache: bfloat16 [8, 65536, 512], P('roll', ('seq', 'tp')), may hold values from -16 to 16
- value_cache: bfloat16 [8, 65536, 512], P('roll', ('seq', 'tp')), may hold values from -16 to 16
- cache_len: int32 [8], P('roll'), may hold values from 32768 to 65536, as said below
- block_pos: int32 [8, 128], P('roll', ('seq', 'tp')), may hold values from 0 to 16383, as said below
Outputs:
- attended: bfloat16 [8, 3584], P('roll')
- fresh_kv: bfloat16 [8, 1024], P('roll')
- served_qkv: bfloat16 [3584, 4096], P(None, 'tp')
- served_out: bfloat16 [3584, 2048], P(None, 'tp')
Inputs may be any that keep to these rules, and one draw needn't show every extreme that they name: `cache_len`: in every draw one rollout has all 65536 positions cached. With i = cache_len[r] mod 8192, and c the 8192-position stretch that holds position cache_len[r]: block_pos[r, b] is i where block b lies in c, i + 8192 where it lies in a later stretch or in the stretch just before c, and 16383 elsewhere.
All inputs are finite; a program needn't handle non-finite values.
Results may differ from a plain program's by a relative error of at most 0.009.
Values may be sent and summed in bfloat16 or wider, within the bound.
A program may use at most 128 MiB of HBM per device.

v0:
```python
import jax
import jax.numpy as jnp
import numpy as np
from jax import lax
from jax.sharding import Mesh
from jax.sharding import PartitionSpec as P

HQ = 16
KVH = 4
HD = 128
BLOCK = 512
STRETCH = 8192
TP = ("tp_0", "tp_1")
SEQ = ("seq_0", "seq_1")
SEQ_TP = ("seq_0", "seq_1", "tp_0", "tp_1")
SEQ_TP_ROLL = ("seq_0", "seq_1", "tp_0", "tp_1", "roll")


rope_base = 10000000.0
norm_eps = 1e-06
floor_score = -1e30


def from_everyone(array, axis):
    copies = jnp.broadcast_to(array, (lax.axis_size(axis), *array.shape))
    return lax.all_to_all(copies, axis, split_axis=0, concat_axis=0, tiled=True)


def joined_along(parts, dim):
    dims = list(parts.shape[1:])
    dims[dim] *= parts.shape[0]
    return jnp.moveaxis(parts, 0, dim).reshape(dims)


def gather_directly(array, axis, dim):
    parts = from_everyone(array, axis)
    return joined_along(parts, dim)


def side_by_side(arrays, axis, dim, along):
    both = jnp.concatenate(arrays, axis=along)
    whole, at, outs = (gather_directly(both, axis, dim), 0, [])
    for a in arrays:
        outs.append(lax.slice_in_dim(whole, at, at + a.shape[along], axis=along))
        at += a.shape[along]
    return tuple(outs)


def side_by_side_2(arrays, axis, split_dim, concat_dim, along):
    widths = [a.shape[along] for a in arrays]
    both = jnp.concatenate(arrays, axis=along)
    whole = lax.all_to_all(both, axis, split_axis=split_dim, concat_axis=concat_dim, tiled=True)
    return tuple(jnp.split(whole, [sum(widths[:k]) for k in range(1, len(widths))], axis=along))


def side_by_side_3(arrays, axis, dim, along):
    both = jnp.concatenate(arrays, axis=along)
    whole, at, outs = (lax.all_gather(both, axis, axis=dim, tiled=True), 0, [])
    for a in arrays:
        outs.append(lax.slice_in_dim(whole, at, at + a.shape[along], axis=along))
        at += a.shape[along]
    return tuple(outs)


def gathered_once(array, axis):
    leaves = jax.tree.leaves(array)
    turns = sorted(range(len(leaves)), key=lambda k: -leaves[k].size)
    width = (1, *leaves[turns[0]].shape)[-1]
    lines = [
        jnp.pad(leaves[k].reshape(-1), (0, -leaves[k].size % width)).reshape(-1, width)
        for k in turns
    ]
    both, at, found = (lax.all_gather(jnp.concatenate(lines), axis), 0, {})
    for k, line in zip(turns, lines):
        piece = both[:, at : at + len(line)].reshape(len(both), -1)
        found[k] = piece[:, : leaves[k].size].reshape(-1, *leaves[k].shape)
        at += len(line)
    numbers = iter(range(len(leaves)))
    return jax.tree.map(lambda _: found[next(numbers)], array)


def combined_by_axis(array, axes, combine):
    for axis in axes:
        pieces = gathered_once(array, axis)
        array = jax.tree.map(lambda part: part[0], pieces)
        for k in range(1, lax.axis_size(axis)):
            array = combine(array, jax.tree.map(lambda part: part[k], pieces))
    return array


def of_everyone(array, axis):
    everything = from_everyone(array, axis)
    return jnp.sum(everything, axis=0)


def frequencies(width):
    half_width = width // 2
    exact = rope_base ** (-2.0 * np.arange(half_width) / width)
    octave = np.floor(np.log2(exact))
    quantum = 2.0 ** (8.0 - octave)
    return np.floor(exact * quantum) / quantum


def rotate(vectors, positions):
    half_width = vectors.shape[-1] // 2
    inverse = jnp.asarray(frequencies(vectors.shape[-1]), dtype=jnp.float32)
    angles = positions.astype(jnp.float32)[..., None] * inverse
    cosine = jnp.cos(angles)
    sine_part = jnp.sin(angles)
    front_half = vectors[..., :half_width]
    back_half = vectors[..., half_width:]
    return jnp.concatenate(
        [front_half * cosine - back_half * sine_part, back_half * cosine + front_half * sine_part],
        axis=-1,
    )


def arrange(columns, tp_count):
    lead = columns.shape[:-1]
    per_rank = HQ // tp_count
    query_part = columns[..., : HQ * HD].reshape(lead + (tp_count, per_rank * HD))
    key_part = jnp.repeat(
        columns[..., HQ * HD : (HQ + KVH) * HD].reshape(lead + (KVH, HD)), tp_count // KVH, axis=-2
    )
    value_part = jnp.repeat(
        columns[..., (HQ + KVH) * HD :].reshape(lead + (KVH, HD)), tp_count // KVH, axis=-2
    )
    return jnp.concatenate([query_part, key_part, value_part], axis=-1)


def normalize(row_block, norm_gain):
    wide_rows = row_block.astype(jnp.float32)
    scaled = wide_rows * lax.rsqrt(
        jnp.mean(wide_rows * wide_rows, axis=1, keepdims=True) + norm_eps
    )
    return (scaled * norm_gain.astype(jnp.float32)).astype(jnp.bfloat16)


def combine_partial(earlier, later):
    top_score = jnp.maximum(earlier[0], later[0])
    left_factor = jnp.exp(earlier[0] - top_score)
    right_factor = jnp.exp(later[0] - top_score)
    return (
        top_score,
        earlier[1] * left_factor + later[1] * right_factor,
        earlier[2] * left_factor[..., None] + later[2] * right_factor[..., None],
    )


def body(
    hidden,
    norm_gain,
    qkv_bias,
    qkv_weight,
    out_weight,
    key_cache,
    value_cache,
    cache_len,
    block_pos,
):
    tp_count = lax.axis_size(TP)
    tp_index = lax.axis_index(TP)
    head_cols = out_weight.shape[1]
    rollouts = hidden.shape[0]
    group_size = HQ // KVH
    score_scale = HD ** (-0.5)
    per_rank = HQ // tp_count
    served_width = (per_rank + 2) * HD
    head_width = head_cols // tp_count
    paired = side_by_side((qkv_weight, out_weight), "roll", 0, 1)
    pair_rows = paired[0].shape[0]
    qkv_blocks = arrange(paired[0], tp_count)
    out_blocks = paired[1].reshape(pair_rows, tp_count, head_width)
    traded = side_by_side_2((qkv_blocks, out_blocks), TP, 1, 0, 2)
    traded_qkv = traded[0].reshape(tp_count * pair_rows, served_width)
    traded_out = traded[1].reshape(tp_count * pair_rows, head_width)
    served_qkv, served_out = side_by_side_3((traded_qkv, traded_out), SEQ, 0, 1)
    bias_wide = qkv_bias.astype(jnp.float32)
    normed = normalize(hidden, norm_gain)
    bias_grouped = arrange(bias_wide, tp_count)
    own_bias = lax.dynamic_slice_in_dim(bias_grouped, tp_index, 1, 0).reshape(served_width)
    local_cols = jnp.dot(normed, served_qkv, preferred_element_type=jnp.float32) + own_bias
    gathered = gather_directly(local_cols.astype(jnp.bfloat16), TP, 1)
    grouped_cols = gathered.reshape(rollouts, tp_count, served_width)
    repeat_count = tp_count // KVH
    queries = grouped_cols[:, :, : per_rank * HD].reshape(rollouts, HQ, HD).astype(jnp.float32)
    new_keys = grouped_cols[:, ::repeat_count, per_rank * HD : (per_rank + 1) * HD].astype(
        jnp.float32
    )
    fresh_value = grouped_cols[:, ::repeat_count, (per_rank + 1) * HD :]
    intra_pos = cache_len % STRETCH
    fresh_key = rotate(new_keys, jnp.broadcast_to(intra_pos[:, None], (rollouts, KVH))).astype(
        jnp.bfloat16
    )
    self_query = rotate(queries, jnp.broadcast_to(intra_pos[:, None], (rollouts, HQ))).astype(
        jnp.bfloat16
    )
    self_score = score_scale * jnp.einsum(
        "rkgd,rkd->rkg",
        self_query.reshape(rollouts, KVH, group_size, HD),
        fresh_key,
        preferred_element_type=jnp.float32,
    )
    blocks = block_pos.shape[1]
    block_query = rotate(
        queries[:, None], jnp.broadcast_to(block_pos[:, :, None], (rollouts, blocks, HQ))
    ).astype(jnp.bfloat16)
    cached_keys = key_cache.reshape(rollouts, blocks, BLOCK, KVH, HD)
    cached_values = value_cache.reshape(rollouts, blocks, BLOCK, KVH, HD)
    scores = score_scale * jnp.einsum(
        "rbkgd,rbpkd->rkgbp",
        block_query.reshape(rollouts, blocks, KVH, group_size, HD),
        cached_keys,
        preferred_element_type=jnp.float32,
    )
    shard_start = lax.axis_index(SEQ_TP) * key_cache.shape[1]
    positions = shard_start + jnp.arange(key_cache.shape[1], dtype=jnp.int32).reshape(blocks, BLOCK)
    valid_mask = (positions[None] < cache_len[:, None, None])[:, None, None]
    masked = jnp.where(valid_mask, scores, floor_score)
    local_max = jnp.max(masked, axis=(3, 4))
    weights = jnp.where(valid_mask, jnp.exp(masked - local_max[..., None, None]), 0.0)
    local_sum = jnp.sum(weights, axis=(3, 4))
    local_out = jnp.einsum(
        "rkgbp,rbpkd->rkgd",
        weights.astype(jnp.bfloat16),
        cached_values,
        preferred_element_type=jnp.float32,
    )
    total_max, total_sum, total_out = combined_by_axis(
        (local_max, local_sum, local_out), SEQ_TP, combine_partial
    )
    top_score = jnp.maximum(total_max, self_score)
    old_factor = jnp.exp(total_max - top_score)
    fresh_weight = jnp.exp(self_score - top_score)
    fresh_rounded = lax.optimization_barrier(fresh_weight.astype(jnp.bfloat16)).astype(jnp.float32)
    denominator = total_sum * old_factor + fresh_weight
    numerator = (
        total_out * old_factor[..., None]
        + fresh_rounded[..., None] * fresh_value.astype(jnp.float32)[:, :, None, :]
    )
    attention = (numerator / denominator[..., None]).reshape(rollouts, HQ * HD).astype(jnp.bfloat16)
    own_heads = lax.dynamic_slice_in_dim(attention, tp_index * head_width, head_width, 1)
    partial_out = lax.dot_general(
        own_heads, served_out, (((1,), (1,)), ((), ())), preferred_element_type=jnp.float32
    )
    attended = of_everyone(partial_out, TP).astype(jnp.bfloat16)
    fresh_kv = jnp.concatenate(
        [fresh_key.reshape(rollouts, KVH * HD), fresh_value.reshape(rollouts, KVH * HD)], axis=1
    )
    return (attended, fresh_kv, served_qkv, served_out)


def solution(mesh):
    finer = Mesh(
        mesh.devices.reshape(2, 4, 4, 2, mesh.shape["roll"]),
        ("seq_0", "seq_1", "tp_0", "tp_1", "roll"),
    )
    in_specs = (
        P("roll", None),
        P(),
        P(),
        P(SEQ_TP_ROLL, None),
        P(SEQ_TP_ROLL, None),
        P("roll", SEQ_TP, None),
        P("roll", SEQ_TP, None),
        P("roll"),
        P("roll", SEQ_TP),
    )
    out_specs = (P("roll", None), P("roll", None), P(None, TP), P(None, TP))
    return jax.shard_map(body, mesh=finer, in_specs=in_specs, out_specs=out_specs, check_vma=False)
```

profile of v0, /device:TPU:1, one launch (start us, length us, event | category | flops | bytes accessed | tf_op | source)
XLA Modules:
  0.0 193.7 jit_solution(462823880561776094)
XLA Ops:
  7.2 0.0 all-gather.10.cloned.1.call-start
  7.2 1.0 pad_maximum_fusion.2
  8.3 14.7 %all_to_all.33 = bf16[2,28,5120]{2,1,0:T(8,128)(2,1)S(1)} all-to-all(bf16[2,28,5120]{2,1,0:T(8,128)(2,1)S(1)} %broadcast_in_dim.32), channel_id=1, replica_groups=mesh['seq_0'=2,'seq_1'=4,'tp_0'=4,'tp_1'=2,'roll'=2] {'roll'}, dimensions={0} | all-to-all | bytes 1146880 | tf_op jit(solution)/shard_map/all_to_all | solution.py:26
  22.9 0.1 reshape.603
  23.3 0.1 broadcast_in_dim.33
  23.4 0.1 broadcast_in_dim.38
  23.4 0.0 copy-start.3
  23.4 0.0 copy-start.4
  23.5 0.0 copy-start.2
  23.5 0.0 copy-start.7
  23.5 0.1 pad_maximum_fusion
  23.6 0.1 copy.53
  23.7 17.3 %all_to_all.34 = bf16[56,8,768]{2,0,1:T(8,128)(2,1)S(1)} all-to-all(bf16[56,8,768]{2,0,1:T(8,128)(2,1)S(1)} %copy.53), channel_id=1, replica_groups=mesh['seq_0'=2,'seq_1'=4,'tp_0'=4,'tp_1'=2,'roll'=2] {'tp_0','tp_1'}, dimensions={1} | all-to-all | bytes 1376256 | tf_op jit(solution)/shard_map/all_to_all | solution.py:52
  41.0 0.9 pad_maximum_fusion.1
  41.9 0.0 all-gather.10.cloned.1.call-update
  42.1 0.1 fusion.28
  42.3 0.1 broadcast_compare_fusion
  42.4 62.7 %all-gather.10.cloned.1.call-done = bf16[3584,768]{1,0:T(8,128)(2,1)} async-done(((bf16[448,768]{1,0:T(8,128)(2,1)}), bf16[3584,768]{1,0:T(8,128)(2,1)}) %all-gather.10.cloned.1.call-update) | async-done | bytes 5505040 | tf_op jit(solution)/shard_map/all_gather | solution.py:58
  105.1 2.3 %slice.373 = bf16[3584,512]{1,0:T(8,128)(2,1)S(1)} slice(bf16[3584,768]{1,0:T(8,128)(2,1)} %all-gather.10.cloned.1.call-done), slice={[0:3584], [0:512]} | slice | bytes 7340032 | tf_op jit(solution)/shard_map/slice | solution.py:60
  107.4 0.0 copy-start
  107.4 0.0 copy-start.6
  107.4 1.8 copy-done
  109.2 0.6 fusion.13
  109.8 0.6 broadcast_in_dim.41
  110.5 5.1 %all-to-all-start.2 = ((bf16[8,4,512]{2,1,0:T(4,128)(2,1)}), bf16[8,4,512]{2,1,0:T(4,128)(2,1)S(1)}, u32[]{:S(2)}, u32[]{:S(2)}) async-start(bf16[8,4,512]{2,1,0:T(4,128)(2,1)} %broadcast_in_dim.41), calls=%async_computation.2 | async-start | bytes 65536 | tf_op jit(solution)/shard_map/all_to_all | solution.py:26
  115.6 0.1 copy.55
  115.7 6.9 %reshape.614 = bf16[4,2,512,4,128]{4,3,2,1,0:T(4,128)(2,1)} reshape(bf16[4,1024,512]{2,1,0:T(8,128)(2,1)} %param.17) | data formatting | bytes 8388608 | tf_op jit(solution)/shard_map/reshape | solution.py:208
  122.6 6.9 %reshape.615 = bf16[4,2,512,4,128]{4,3,2,1,0:T(4,128)(2,1)} reshape(bf16[4,1024,512]{2,1,0:T(8,128)(2,1)} %param.18) | data formatting | bytes 8388608 | tf_op jit(solution)/shard_map/reshape | solution.py:209
  129.5 1.6 slice.404
  131.2 0.0 copy-start.1
  131.3 0.1 fusion.127
  131.4 0.2 fusion.25
  131.6 3.7 %fusion.128 = (f32[4,4,4]{2,1,0:T(4,128)S(1)}, f32[4,4,4,2,512]{4,2,3,1,0:T(4,128)S(1)}) fusion(bf16[4,2,512,4,128]{4,3,2,1,0:T(4,128)(2,1)} %reshape.614, bf16[4,2,4,4,64]{4,3,1,2,0:T(4,128)(2,1)S(1)} %get-tuple-element.47, bf16[4,2,4,4,64]{4,3,1,2,0:T(4,128)(2,1)S(1)} %get-tuple-element.46, pred[4,2,512]{2,1,0:T(4,128)(4,1)S(1)} %broadcast_compare_fusion), kind=kOutput, calls=%fused_computation.209 | convolution fusion | flops 17039296 | bytes 4493568 | tf_op jit(solution)/shard_map/rbkgd,rbpkd->rkgbp/dot_general | solution.py:210
  135.3 0.1 reshape.617
  135.4 0.3 fusion.14
  135.7 0.1 reshape.619
  135.8 3.0 %fusion = f32[4,4,4,128,1]{3,2,4,1,0:T(4,128)S(1)} fusion(bf16[4,2,512,4,128]{4,3,2,1,0:T(4,128)(2,1)} %reshape.615, f32[4,4,4,2,512]{4,2,3,1,0:T(4,128)S(1)} %get-tuple-element.58, f32[4,4,4]{2,1,0:T(4,128)S(1)} %get-tuple-element.57, pred[4,2,512]{2,1,0:T(4,128)(4,1)S(1)} %broadcast_compare_fusion), kind=kOutput, calls=%fused_computation | convolution fusion | flops 16973824 | bytes 4493568 | tf_op jit(solution)/shard_map/rkgbp,rbpkd->rkgd/dot_general | solution.py:223
  138.8 3.5 %all-gather.4 = f32[2,66,128]{2,1,0:T(8,128)S(1)} all-gather(f32[1,66,128]{2,1,0:T(8,128)S(1)} %maximum_bitcast_fusion), channel_id=2, replica_groups=mesh['seq_0'=2,'seq_1'=4,'tp_0'=4,'tp_1'=2,'roll'=2] {'seq_0'}, dimensions={0}, use_global_device_ids=true | all-gather | bytes 101376 | tf_op jit(solution)/shard_map/all_gather | solution.py:73
  142.3 0.1 fusion.58
  142.4 9.1 %all-gather.5 = f32[4,66,128]{2,1,0:T(8,128)S(1)} all-gather(f32[1,66,128]{2,1,0:T(8,128)S(1)} %maximum_bitcast_fusion.1), channel_id=3, replica_groups=mesh['seq_0'=2,'seq_1'=4,'tp_0'=4,'tp_1'=2,'roll'=2] {'seq_1'}, dimensions={0}, use_global_device_ids=true | all-gather | bytes 168960 | tf_op jit(solution)/shard_map/all_gather | solution.py:73
  151.6 0.1 fusion.49
  151.8 9.6 %all-gather.6 = f32[4,66,128]{2,1,0:T(8,128)S(1)} all-gather(f32[1,66,128]{2,1,0:T(8,128)S(1)} %maximum_bitcast_fusion.2), channel_id=4, replica_groups=mesh['seq_0'=2,'seq_1'=4,'tp_0'=4,'tp_1'=2,'roll'=2] {'tp_0'}, dimensions={0}, use_global_device_ids=true | all-gather | bytes 168960 | tf_op jit(solution)/shard_map/all_gather | solution.py:73
  161.4 0.1 fusion.40
  161.6 8.8 %all-gather.7 = f32[2,66,128]{2,1,0:T(8,128)S(1)} all-gather(f32[1,66,128]{2,1,0:T(8,128)S(1)} %maximum_bitcast_fusion.3), channel_id=5, replica_groups=mesh['seq_0'=2,'seq_1'=4,'tp_0'=4,'tp_1'=2,'roll'=2] {'tp_1'}, dimensions={0}, use_global_device_ids=true | all-gather | bytes 101376 | tf_op jit(solution)/shard_map/all_gather | solution.py:73
  170.5 0.1 fusion.71
  170.6 0.1 fusion.36
  170.8 0.1 squeeze.142
  170.9 0.1 squeeze.143
  171.0 0.1 squeeze.139
  171.1 0.1 squeeze.140
  171.2 0.1 fusion.132
  171.3 0.2 fusion.66
  171.5 0.1 broadcast_multiply_fusion
  171.6 0.1 div.15
  171.8 0.1 mul.454
  171.9 0.1 mul.457
  172.0 0.1 mul.476
  172.1 0.6 fusion.78
  172.7 0.8 broadcast_in_dim.44
  173.5 4.0 %all-to-all-start.3 = ((f32[8,4,3584]{2,1,0:T(4,128)}), f32[8,4,3584]{2,1,0:T(4,128)S(1)}, u32[]{:S(2)}, u32[]{:S(2)}) async-start(f32[8,4,3584]{2,1,0:T(4,128)} %broadcast_in_dim.44), calls=%async_computation.3 | async-start | bytes 917504 | tf_op jit(solution)/shard_map/all_to_all | solution.py:26
  177.6 0.1 fusion.131
  177.6 0.6 pad_maximum_fusion.5
  178.2 8.0 %all-to-all-done.3 = f32[8,4,3584]{2,1,0:T(4,128)S(1)} async-done(((f32[8,4,3584]{2,1,0:T(4,128)}), f32[8,4,3584]{2,1,0:T(4,128)S(1)}, u32[]{:S(2)}, u32[]{:S(2)}) %all-to-all-start.3) | async-done | bytes 458784 | tf_op jit(solution)/shard_map/all_to_all | solution.py:26
  186.2 0.7 reduce_sum.29
  (69 shorter events, 0.9 us)
Async XLA Ops:
  7.2 97.9 %all-gather.10.cloned.1.call-start = ((), (), s32[]{:S(2)}) async-start(), calls=%async_computation.4 | async-start | bytes 6193152 | tf_op jit(solution)/shard_map/all_gather | solution.py:58
  23.4 18.5 %copy-start.3 = (bf16[3072]{0:T(1024)(128)(2,1)S(1)}, bf16[3072]{0:T(1024)(128)(2,1)}, u32[]{:S(2)}) copy-start(bf16[3072]{0:T(1024)(128)(2,1)} %param.14) | copy-start | bytes 18436
  23.4 18.6 %copy-start.4 = (bf16[3584]{0:T(1024)(128)(2,1)S(1)}, bf16[3584]{0:T(1024)(128)(2,1)}, u32[]{:S(2)}) copy-start(bf16[3584]{0:T(1024)(128)(2,1)} %param.13) | copy-start | bytes 21508
  23.5 18.6 %copy-start.2 = (bf16[4,3584]{1,0:T(4,128)(2,1)S(1)}, bf16[4,3584]{1,0:T(4,128)(2,1)}, u32[]{:S(2)}) copy-start(bf16[4,3584]{1,0:T(4,128)(2,1)} %param.12) | copy-start | bytes 86020
  23.5 18.8 %copy-start.7 = (s32[4]{0:T(128)S(1)}, s32[4]{0:T(128)}, u32[]{:S(2)}) copy-start(s32[4]{0:T(128)} %param.19) | copy-start | bytes 52
  107.4 1.8 copy-start
  107.4 8.2 %copy-start.6 = (s32[4,2]{0,1:T(2,128)S(1)}, s32[4,2]{0,1:T(2,128)}, u32[]{:S(2)}) copy-start(s32[4,2]{0,1:T(2,128)} %param.20) | copy-start | bytes 100
  110.5 20.7 %all-to-all-start.2 = ((bf16[8,4,512]{2,1,0:T(4,128)(2,1)}), bf16[8,4,512]{2,1,0:T(4,128)(2,1)S(1)}, u32[]{:S(2)}, u32[]{:S(2)}) async-start(bf16[8,4,512]{2,1,0:T(4,128)(2,1)} %broadcast_in_dim.41), calls=%async_computation.2 | async-start | bytes 65536 | tf_op jit(solution)/shard_map/all_to_all | solution.py:26
  129.5 1.8 copy-start.5
  131.2 41.0 %copy-start.1 = (bf16[3584,256]{1,0:T(8,128)(2,1)}, bf16[3584,256]{1,0:T(8,128)(2,1)S(1)}, u32[]{:S(2)}) copy-start(bf16[3584,256]{1,0:T(8,128)(2,1)S(1)} %slice.404) | copy-start | bytes 5505028
  173.5 12.6 %all-to-all-start.3 = ((f32[8,4,3584]{2,1,0:T(4,128)}), f32[8,4,3584]{2,1,0:T(4,128)S(1)}, u32[]{:S(2)}, u32[]{:S(2)}) async-start(f32[8,4,3584]{2,1,0:T(4,128)} %broadcast_in_dim.44), calls=%async_computation.3 | async-start | bytes 917504 | tf_op jit(solution)/shard_map/all_to_all | solution.py:26
Sparse Core Ops, SparseCore 0:
  42.1 62.9 all-gather.9
where the time goes:
time: 195 us; the launch traced here: 194 us
  waiting for transfers between devices  70.7 us (36%)
  blocking collectives  63 us (32%)
  local copies, waits for them, and re-layouts  23.1 us (12%)
  between operations  14.6 us (7%)
  starting transfers between devices  9.16 us (5%)
  matrix products  8.1 us (4%)
  other arithmetic  5.03 us (3%)
    all_gather x1, waiting for transfers between devices, side_by_side_3(): whole, at, outs = (lax.all_gather(both, axis, axis=dim, tiled=True), 0, [])  62.7 us
    all_gather x4, blocking collectives, gathered_once(): both, at, found = (lax.all_gather(jnp.concatenate(lines), axis), 0, {})  31.1 us
    all_to_all x1, blocking collectives, side_by_side_2(): lax.all_to_all(both, axis, split_axis=split_dim, concat_axis=concat_dim,...  17.3 us
    all_to_all x1, blocking collectives, from_everyone(): return lax.all_to_all(copies, axis, split_axis=0, concat_axis=0, tiled=True)  14.7 us
    all_to_all x2, starting transfers between devices, from_everyone(): return lax.all_to_all(copies, axis, split_axis=0, concat_axis=0, tiled=True)  9.13 us
    all_to_all x2, waiting for transfers between devices, from_everyone(): return lax.all_to_all(copies, axis, split_axis=0, concat_axis=0, tiled=True)  7.95 us
    reshape x1, local copies, waits for them, and re-layouts, body(): cached_values = value_cache.reshape(rollouts, blocks, BLOCK, KVH, HD)  6.91 us
    reshape x1, local copies, waits for them, and re-layouts, body(): cached_keys = key_cache.reshape(rollouts, blocks, BLOCK, KVH, HD)  6.9 us
  transfers between devices with their start and end apart: 3, of which 2 were waited for; matrix products, arithmetic and copies ran while one was open for 9% of the time, Pallas kernels for 0%

commit v1 on v0

--- a/solution.py
+++ b/solution.py
@@ -2,6 +2,8 @@
 import jax.numpy as jnp
 import numpy as np
 from jax import lax
+from jax.experimental import pallas as pl
+from jax.experimental.pallas import tpu as pltpu
 from jax.sharding import Mesh
 from jax.sharding import PartitionSpec as P
 
@@ -19,6 +21,160 @@
 rope_base = 10000000.0
 norm_eps = 1e-06
 floor_score = -1e30
+
+
+MESH = pl.DeviceIdType.MESH
+WAVES = (0, 1, 3, 2)
+GROUPS = 7
+
+
+def place():
+    x = lax.axis_index("roll") * 2 + lax.axis_index("seq_0")
+    return x, lax.axis_index("tp_0"), lax.axis_index("seq_1"), lax.axis_index("tp_1")
+
+
+def device(x, y, z, core):
+    return (x % 2, z, y, core, x // 2)
+
+
+def relay_kernel(src_ref, w_ref, own_sem, trade_send, trade_recv, ring_send, ring_recv):
+    x, y, z, core = place()
+
+    def remote(src, dst, send, recv, target):
+        return pltpu.make_async_remote_copy(
+            src_ref=src, dst_ref=dst, send_sem=send, recv_sem=recv,
+            device_id=device(*target), device_id_type=MESH,
+        )
+
+    def slot(bx, bz, tiles, first, count):
+        return w_ref.at[pl.ds(*tiles), (bx % 2) * 4 + bz, pl.ds(first, count), bx // 2]
+
+    barrier = pltpu.get_barrier_semaphore()
+    partners = [(x, (y + dy) % 4, z, (core + dc) % 2) for dy in range(4) for dc in range(2) if dy + dc > 0]
+    partners += [((x + d) % 4, y, z, core) for d in (1, 3)]
+    partners += [(x, y, (z + d) % 4, core) for d in (1, 3)]
+    for partner in partners:
+        pl.semaphore_signal(barrier, inc=1, device_id=device(*partner), device_id_type=MESH)
+    pl.semaphore_wait(barrier, len(partners))
+
+    def traded(dy, dc):
+        there = ((y + dy) % 4, (core + dc) % 2)
+        return remote(
+            src_ref.at[there[0] * 2 + there[1]],
+            w_ref.at[:, (x % 2) * 4 + z, y * 2 + core, x // 2],
+            trade_send.at[dy * 2 + dc], trade_recv.at[dy * 2 + dc],
+            (x, there[0], z, there[1]),
+        )
+
+    def arrived(dy, dc):
+        from_tp = ((y - dy) % 4) * 2 + (core + dc) % 2
+        here = w_ref.at[:, (x % 2) * 4 + z, from_tp, x // 2]
+        return remote(here, here, trade_send.at[dy * 2 + dc], trade_recv.at[dy * 2 + dc],
+                      (x, (y + dy) % 4, z, (core + dc) % 2))
+
+    own = pltpu.make_async_copy(
+        src_ref.at[y * 2 + core], w_ref.at[:, (x % 2) * 4 + z, y * 2 + core, x // 2], own_sem
+    )
+    traded(0, 1).start()
+    own.start()
+    for dy in (3, 1, 2):
+        for dc in (0, 1):
+            traded(dy, dc).start()
+
+    def ring(wave, half, kind, f, g, part, step):
+        first = ((y + WAVES[wave]) % 4) * 2
+        tiles = (half * 3, 3)
+        df, dg = step
+        if half == 0:
+            bx, bz, tx, tz = x + g, z + f, x + dg, z + df
+        else:
+            bx, bz, tx, tz = x + f, z + g, x + df, z + dg
+        bx, bz, tx, tz = bx % 4, bz % 4, tx % 4, tz % 4
+        block = slot(bx, bz, tiles, first + (0 if part is None else part), 2 if part is None else 1)
+        return remote(block, block, ring_send.at[wave], ring_recv.at[wave, half * 20 + kind], (tx, y, tz, core))
+
+    order = (0, -1, 1, 2)
+
+    def sideways(wave, half, f):
+        k = 4 + order.index(f) * 4
+        ring(wave, half, k, f, 0, None, (0, 1)).start()
+        ring(wave, half, k + 1, f, 0, None, (0, -1)).start()
+
+    def s1(wave):
+        if wave == 0:
+            own.wait()
+            arrived(0, 1).wait_recv()
+        else:
+            dy = (-WAVES[wave]) % 4
+            arrived(dy, 0).wait_recv()
+            arrived(dy, 1).wait_recv()
+        for half in (0, 1):
+            ring(wave, half, 0, 0, 0, None, (1, 0)).start()
+            ring(wave, half, 1, 0, 0, None, (-1, 0)).start()
+        for half in (0, 1):
+            sideways(wave, half, 0)
+
+    def s2(wave):
+        for half in (0, 1):
+            ring(wave, half, 0, -1, 0, None, (1, 0)).wait_recv()
+            ring(wave, half, 2, -1, 0, 0, (1, 0)).start()
+            ring(wave, half, 1, 1, 0, None, (1, 0)).wait_recv()
+            ring(wave, half, 3, 1, 0, 1, (-1, 0)).start()
+        for half in (0, 1):
+            sideways(wave, half, -1)
+            sideways(wave, half, 1)
+
+    def s3(wave):
+        for half in (0, 1):
+            ring(wave, half, 2, 2, 0, 0, (1, 0)).wait_recv()
+            ring(wave, half, 3, 2, 0, 1, (1, 0)).wait_recv()
+            sideways(wave, half, 2)
+
+    def s4(wave):
+        for f in order:
+            for half in (0, 1):
+                k = 4 + order.index(f) * 4
+                ring(wave, half, k, f, -1, None, (0, 1)).wait_recv()
+                ring(wave, half, k + 2, f, -1, 0, (0, 1)).start()
+                ring(wave, half, k + 1, f, 1, None, (0, 1)).wait_recv()
+                ring(wave, half, k + 3, f, 1, 1, (0, -1)).start()
+
+    def s5(wave):
+        for f in order:
+            for half in (0, 1):
+                k = 4 + order.index(f) * 4
+                ring(wave, half, k + 2, f, 2, 0, (0, 1)).wait_recv()
+                ring(wave, half, k + 3, f, 2, 1, (0, 1)).wait_recv()
+        sent = w_ref.at[:, 0:5, 0:6, 0]
+        remote(sent, sent, ring_send.at[wave], ring_recv.at[wave, 0], (x, y, (z + 1) % 4, core)).wait_send()
+
+    for step, wave in ((s1, 0), (s1, 1), (s2, 0), (s3, 0), (s1, 2), (s2, 1), (s4, 0), (s3, 1), (s1, 3),
+                       (s2, 2), (s4, 1), (s3, 2), (s2, 3), (s4, 2), (s3, 3), (s4, 3)):
+        step(wave)
+    for wave in range(4):
+        s5(wave)
+    for dy in range(4):
+        for dc in (0, 1):
+            if dy + dc > 0:
+                traded(dy, dc).wait_send()
+
+
+def relay(src):
+    return pl.pallas_call(
+        relay_kernel,
+        name="relay",
+        out_shape=jax.ShapeDtypeStruct((6, 8, 8, 2, GROUPS, 4, HD), jnp.bfloat16),
+        in_specs=[pl.BlockSpec(memory_space=pltpu.HBM)],
+        out_specs=pl.BlockSpec(memory_space=pltpu.VMEM),
+        scratch_shapes=[
+            pltpu.SemaphoreType.DMA,
+            pltpu.SemaphoreType.DMA((8,)),
+            pltpu.SemaphoreType.DMA((8,)),
+            pltpu.SemaphoreType.DMA((4,)),
+            pltpu.SemaphoreType.DMA((4, 40)),
+        ],
+        compiler_params=pltpu.CompilerParams(collective_id=0, has_side_effects=True, vmem_limit_bytes=30 * 2**20),
+    )(src)
 
 
 def from_everyone(array, axis):
@@ -126,6 +282,14 @@
         columns[..., (HQ + KVH) * HD :].reshape(lead + (KVH, HD)), tp_count // KVH, axis=-2
     )
     return jnp.concatenate([query_part, key_part, value_part], axis=-1)
+
+
+def arrange_tiles(qkv_rows, out_rows):
+    rows = qkv_rows.shape[0]
+    tiles = jnp.concatenate([qkv_rows, out_rows], axis=1).reshape(rows, 40, HD)
+    order = [[2 * t, 2 * t + 1, 16 + t // 2, 20 + t // 2, 24 + 2 * t, 25 + 2 * t] for t in range(8)]
+    picked = jnp.stack([jnp.stack([tiles[:, k] for k in row]) for row in order])
+    return picked.reshape(8, 6, GROUPS, 4, HD)
 
 
 def normalize(row_block, norm_gain):
@@ -167,14 +331,10 @@
     per_rank = HQ // tp_count
     served_width = (per_rank + 2) * HD
     head_width = head_cols // tp_count
-    paired = side_by_side((qkv_weight, out_weight), "roll", 0, 1)
-    pair_rows = paired[0].shape[0]
-    qkv_blocks = arrange(paired[0], tp_count)
-    out_blocks = paired[1].reshape(pair_rows, tp_count, head_width)
-    traded = side_by_side_2((qkv_blocks, out_blocks), TP, 1, 0, 2)
-    traded_qkv = traded[0].reshape(tp_count * pair_rows, served_width)
-    traded_out = traded[1].reshape(tp_count * pair_rows, head_width)
-    served_qkv, served_out = side_by_side_3((traded_qkv, traded_out), SEQ, 0, 1)
+    src = arrange_tiles(qkv_weight, out_weight)
+    joint = relay(src).reshape(6, 3584, HD)
+    served_qkv = jnp.moveaxis(joint[:4], 0, 1).reshape(3584, served_width)
+    served_out = jnp.moveaxis(joint[4:], 0, 1).reshape(3584, head_width)
     bias_wide = qkv_bias.astype(jnp.float32)
     normed = normalize(hidden, norm_gain)
     bias_grouped = arrange(bias_wide, tp_count)

time: 195 us -> 137 us (0.70)
  waiting for transfers between devices: 70.7 us -> 7.95 us
  Pallas kernels: 0 us -> 42.7 us
  blocking collectives: 63 us -> 31.1 us
  between operations: 14.6 us -> 1.3 us
  local copies, waits for them, and re-layouts: 23.1 us -> 28.6 us
  matrix products: 8.1 us -> 10.1 us
    all_gather x1 -> x0, waiting for transfers between devices: 62.7 us -> none  [side_by_side_3(): whole, at, outs = (lax.all_gather(both, axis, axis=dim, tiled=True), 0, [])]
    pallas_call x0 -> x1, Pallas kernels: none -> 42.7 us  [relay(): pl.pallas_call(relay_kernel, name='relay', out_shape=jax.ShapeDtypeStruct...]
    all_to_all x2 -> x0, blocking collectives: 31.9 us -> none  [the longest x1 17.3 us: side_by_side_2(): lax.all_to_all(both, axis, split_axis=split_dim, concat_axis=concat_dim,...]
    reshape x5 -> x3, local copies, waits for them, and re-layouts: 0.22 us -> 4.04 us  [the longest x1 2.47 us: body(): served_qkv = jnp.moveaxis(joint[:4], 0, 1).reshape(3584, served_width)]
    dot_general x1, matrix products: 0.62 us -> 2.66 us  [body(): jnp.dot(normed, served_qkv, preferred_element_type=jnp.float32) + own_bias]
    slice x3 -> x6, local copies, waits for them, and re-layouts: 3.92 us -> 3.32 us  [the longest x1 1.73 us: body(): served_qkv = jnp.moveaxis(joint[:4], 0, 1).reshape(3584, served_width)]
  transfers between devices with their start and end apart: 3 -> 2, of which waited for: 2 -> 1; matrix products, arithmetic and copies ran while one was open for 9% -> 12% of each run, Pallas kernels for 0% -> 0%
where the time goes in v1:
time: 137 us; the launch traced here: 136 us
  Pallas kernels  42.7 us (31%)
  blocking collectives  31.1 us (23%)
  local copies, waits for them, and re-layouts  28.6 us (21%)
  matrix products  10.1 us (7%)
  starting transfers between devices  9.69 us (7%)
  waiting for transfers between devices  7.95 us (6%)
  other arithmetic  4.76 us (3%)
    pallas_call x1, Pallas kernels, relay(): pl.pallas_call(relay_kernel, name='relay', out_shape=jax.ShapeDtypeStruct...  42.7 us
    all_gather x4, blocking collectives, gathered_once(): both, at, found = (lax.all_gather(jnp.concatenate(lines), axis), 0, {})  31.1 us
    all_to_all x2, starting transfers between devices, from_everyone(): return lax.all_to_all(copies, axis, split_axis=0, concat_axis=0, tiled=True)  9.69 us
    all_to_all x2, waiting for transfers between devices, from_everyone(): return lax.all_to_all(copies, axis, split_axis=0, concat_axis=0, tiled=True)  7.95 us
    reshape x1, local copies, waits for them, and re-layouts, body(): cached_values = value_cache.reshape(rollouts, blocks, BLOCK, KVH, HD)  7.04 us
    reshape x1, local copies, waits for them, and re-layouts, body(): cached_keys = key_cache.reshape(rollouts, blocks, BLOCK, KVH, HD)  6.92 us
    dot_general x1, matrix products, body(): jnp.einsum('rbkgd,rbpkd->rkgbp', block_query.reshape(rollouts, blocks, KV...  3.5 us
    dot_general x1, matrix products, body(): jnp.einsum('rkgbp,rbpkd->rkgd', weights.astype(jnp.bfloat16), cached_valu...  3.13 us
  transfers between devices with their start and end apart: 2, of which 1 were waited for; matrix products, arithmetic and copies ran while one was open for 12% of the time, Pallas kernels for 0%

profile of v1, /device:TPU:1, one launch (start us, length us, event | category | flops | bytes accessed | tf_op | source)
XLA Modules:
  0.0 136.1 jit_solution(12200246903475035216)
XLA Ops:
  0.6 1.0 pad_maximum_fusion
  1.7 0.7 slice_reduce_fusion.19
  2.5 0.1 slice_reduce_fusion.38
  2.6 0.8 slice_reduce_fusion
  3.3 0.7 convert_element_type.87
  4.0 0.7 slice.565
  6.2 42.7 %relay.1 = bf16[6,8,8,2,7,4,128]{6,5,4,3,2,1,0:T(4,128)(2,1)S(1)} custom-call(bf16[8,6,7,4,128]{4,3,2,1,0:T(4,128)(2,1)S(1)} %constant_dynamic-update-slice_fusion.src_ref), custom_call_target="tpu_custom_call" | custom-call | tf_op jit(solution)/shard_map/relay/pallas_call | solution.py:163
  48.9 0.0 copy-start
  48.9 2.4 %copy-done = bf16[6,8,8,2,7,4,128]{6,5,4,3,2,1,0:T(4,128)(2,1)} copy-done((bf16[6,8,8,2,7,4,128]{6,5,4,3,2,1,0:T(4,128)(2,1)}, bf16[6,8,8,2,7,4,128]{6,5,4,3,2,1,0:T(4,128)(2,1)S(1)}, u32[]{:S(2)}) %copy-start) | copy-done | bytes 5505048
  51.3 1.7 %slice.462 = bf16[4,8,8,2,7,4,128]{6,5,4,3,2,1,0:T(4,128)(2,1)S(1)} slice(bf16[6,8,8,2,7,4,128]{6,5,4,3,2,1,0:T(4,128)(2,1)S(1)} %relay.1), slice={[0:4], [0:8], [0:8], [0:2], [0:7], [0:4], [0:128]} | slice | bytes 7340032 | tf_op jit(solution)/shard_map/slice | solution.py:336
  53.0 0.0 copy-start.3
  53.0 0.0 copy-start.2
  53.0 0.0 copy-start.6
  53.1 2.5 %copy.407 = bf16[4,448,8,128]{3,2,0,1:T(8,128)(2,1)} copy(bf16[4,448,8,128]{3,2,1,0:T(8,128)(2,1)S(1)} %bitcast.303) | data formatting | bytes 7340032 | tf_op jit(solution)/shard_map/reshape | solution.py:336
  55.5 0.0 copy-done.3
  55.6 0.0 copy-done.2
  55.6 0.1 fusion.28
  55.8 2.7 %fusion.13 = bf16[4,512]{1,0:T(4,128)(2,1)S(1)} fusion(bf16[3584,512]{1,0:T(8,128)(2,1)} %bitcast.301, bf16[4,3584]{1,0:T(4,128)(2,1)S(1)} %copy-done.2, f32[3584]{0:T(1024)S(1)} %convert_element_type.85, f32[4]{0:T(128)S(1)} %add_rsqrt_fusion, f32[512]{0:T(512)S(1)} %bitcast.319), kind=kOutput, calls=%fused_computation.10 | convolution fusion | flops 14741504 | bytes 3719184 | tf_op jit(solution)/shard_map/dot_general | solution.py:342
  58.4 0.6 broadcast_in_dim.28
  59.0 5.7 %all-to-all-start = ((bf16[8,4,512]{2,1,0:T(4,128)(2,1)}), bf16[8,4,512]{2,1,0:T(4,128)(2,1)S(1)}, u32[]{:S(2)}, u32[]{:S(2)}) async-start(bf16[8,4,512]{2,1,0:T(4,128)(2,1)} %broadcast_in_dim.28), calls=%async_computation | async-start | bytes 65536 | tf_op jit(solution)/shard_map/all_to_all | solution.py:182
  64.7 0.0 copy-done.6
  64.7 0.1 broadcast_compare_fusion
  64.8 0.0 copy-done.5
  64.9 0.1 copy.294
  65.0 6.9 %reshape.705 = bf16[4,2,512,4,128]{4,3,2,1,0:T(4,128)(2,1)} reshape(bf16[4,1024,512]{2,1,0:T(8,128)(2,1)} %param.17) | data formatting | bytes 8388608 | tf_op jit(solution)/shard_map/reshape | solution.py:368
  71.9 7.0 %reshape.706 = bf16[4,2,512,4,128]{4,3,2,1,0:T(4,128)(2,1)} reshape(bf16[4,1024,512]{2,1,0:T(8,128)(2,1)} %param.18) | data formatting | bytes 8388608 | tf_op jit(solution)/shard_map/reshape | solution.py:369
  78.9 0.0 slice-done
  78.9 1.5 %copy.408 = bf16[2,448,8,128]{3,2,0,1:T(8,128)(2,1)} copy(bf16[2,448,8,128]{3,2,1,0:T(8,128)(2,1)S(1)} %bitcast.300) | data formatting | bytes 3670016 | tf_op jit(solution)/shard_map/reshape | solution.py:337
  80.5 0.0 all-to-all-done
  80.6 0.1 fusion.125
  80.6 0.0 copy-done.4
  80.6 0.2 fusion.25
  80.9 3.5 %fusion.126 = (f32[4,4,4]{2,1,0:T(4,128)S(1)}, f32[4,4,4,2,512]{4,2,3,1,0:T(4,128)S(1)}) fusion(bf16[4,2,512,4,128]{4,3,2,1,0:T(4,128)(2,1)} %reshape.705, bf16[4,2,4,4,64]{4,3,1,2,0:T(4,128)(2,1)S(1)} %get-tuple-element.83, bf16[4,2,4,4,64]{4,3,1,2,0:T(4,128)(2,1)S(1)} %get-tuple-element.82, pred[4,2,512]{2,1,0:T(4,128)(4,1)S(1)} %broadcast_compare_fusion), kind=kOutput, calls=%fused_computation.293 | convolution fusion | flops 17039296 | bytes 4493568 | tf_op jit(solution)/shard_map/rbkgd,rbpkd->rkgbp/dot_general | solution.py:370
  84.4 0.1 reshape.708
  84.5 0.3 fusion.14
  84.8 3.1 %fusion = f32[4,4,4,128,1]{3,2,4,1,0:T(4,128)S(1)} fusion(bf16[4,2,512,4,128]{4,3,2,1,0:T(4,128)(2,1)} %reshape.706, f32[4,4,4,2,512]{4,2,3,1,0:T(4,128)S(1)} %get-tuple-element.94, f32[4,4,4]{2,1,0:T(4,128)S(1)} %get-tuple-element.93, pred[4,2,512]{2,1,0:T(4,128)(4,1)S(1)} %broadcast_compare_fusion), kind=kOutput, calls=%fused_computation | convolution fusion | flops 16973824 | bytes 4493568 | tf_op jit(solution)/shard_map/rkgbp,rbpkd->rkgd/dot_general | solution.py:383
  87.9 0.1 reshape.710
  88.0 3.5 %all-gather.4 = f32[2,66,128]{2,1,0:T(8,128)S(1)} all-gather(f32[1,66,128]{2,1,0:T(8,128)S(1)} %maximum_bitcast_fusion), channel_id=2, replica_groups=mesh['seq_0'=2,'seq_1'=4,'tp_0'=4,'tp_1'=2,'roll'=2] {'seq_0'}, dimensions={0}, use_global_device_ids=true | all-gather | bytes 101376 | tf_op jit(solution)/shard_map/all_gather | solution.py:229
  91.6 0.1 fusion.58
  91.7 9.6 %all-gather.5 = f32[4,66,128]{2,1,0:T(8,128)S(1)} all-gather(f32[1,66,128]{2,1,0:T(8,128)S(1)} %maximum_bitcast_fusion.1), channel_id=3, replica_groups=mesh['seq_0'=2,'seq_1'=4,'tp_0'=4,'tp_1'=2,'roll'=2] {'seq_1'}, dimensions={0}, use_global_device_ids=true | all-gather | bytes 168960 | tf_op jit(solution)/shard_map/all_gather | solution.py:229
  101.3 0.1 fusion.49
  101.4 9.2 %all-gather.6 = f32[4,66,128]{2,1,0:T(8,128)S(1)} all-gather(f32[1,66,128]{2,1,0:T(8,128)S(1)} %maximum_bitcast_fusion.2), channel_id=4, replica_groups=mesh['seq_0'=2,'seq_1'=4,'tp_0'=4,'tp_1'=2,'roll'=2] {'tp_0'}, dimensions={0}, use_global_device_ids=true | all-gather | bytes 168960 | tf_op jit(solution)/shard_map/all_gather | solution.py:229
  110.7 0.1 fusion.40
  110.8 8.8 %all-gather.7 = f32[2,66,128]{2,1,0:T(8,128)S(1)} all-gather(f32[1,66,128]{2,1,0:T(8,128)S(1)} %maximum_bitcast_fusion.3), channel_id=5, replica_groups=mesh['seq_0'=2,'seq_1'=4,'tp_0'=4,'tp_1'=2,'roll'=2] {'tp_1'}, dimensions={0}, use_global_device_ids=true | all-gather | bytes 101376 | tf_op jit(solution)/shard_map/all_gather | solution.py:229
  119.7 0.1 fusion.71
  119.8 0.1 fusion.36
  120.0 0.1 squeeze.139
  120.1 0.1 squeeze.140
  120.2 0.1 squeeze.142
  120.3 0.1 squeeze.143
  120.4 0.1 fusion.130
  120.4 0.2 fusion.66
  120.7 0.1 broadcast_multiply_fusion
  120.8 0.1 div.15
  121.0 0.1 mul.454
  121.1 0.1 mul.457
  121.2 0.1 mul.476
  121.3 0.6 fusion.78
  121.9 0.8 broadcast_in_dim.35
  122.8 4.0 %all-to-all-start.1 = ((f32[8,4,3584]{2,1,0:T(4,128)}), f32[8,4,3584]{2,1,0:T(4,128)S(1)}, u32[]{:S(2)}, u32[]{:S(2)}) async-start(f32[8,4,3584]{2,1,0:T(4,128)} %broadcast_in_dim.35), calls=%async_computation.1 | async-start | bytes 917504 | tf_op jit(solution)/shard_map/all_to_all | solution.py:182
  126.8 0.1 fusion.129
  126.9 0.6 pad_maximum_fusion.3
  127.5 8.0 %all-to-all-done.1 = f32[8,4,3584]{2,1,0:T(4,128)S(1)} async-done(((f32[8,4,3584]{2,1,0:T(4,128)}), f32[8,4,3584]{2,1,0:T(4,128)S(1)}, u32[]{:S(2)}, u32[]{:S(2)}) %all-to-all-start.1) | async-done | bytes 458784 | tf_op jit(solution)/shard_map/all_to_all | solution.py:182
  135.4 0.7 reduce_sum.29
  (144 shorter events, 1.9 us)
Async XLA Ops:
  48.9 2.4 %copy-start = (bf16[6,8,8,2,7,4,128]{6,5,4,3,2,1,0:T(4,128)(2,1)}, bf16[6,8,8,2,7,4,128]{6,5,4,3,2,1,0:T(4,128)(2,1)S(1)}, u32[]{:S(2)}) copy-start(bf16[6,8,8,2,7,4,128]{6,5,4,3,2,1,0:T(4,128)(2,1)S(1)} %relay.1) | copy-start | bytes 16515076
  53.0 2.5 %copy-start.3 = (bf16[3584]{0:T(1024)(128)(2,1)S(1)}, bf16[3584]{0:T(1024)(128)(2,1)}, u32[]{:S(2)}) copy-start(bf16[3584]{0:T(1024)(128)(2,1)} %param.13) | copy-start | bytes 21508
  53.0 2.5 %copy-start.2 = (bf16[4,3584]{1,0:T(4,128)(2,1)S(1)}, bf16[4,3584]{1,0:T(4,128)(2,1)}, u32[]{:S(2)}) copy-start(bf16[4,3584]{1,0:T(4,128)(2,1)} %param.12) | copy-start | bytes 86020
  53.0 11.7 %copy-start.6 = (s32[4]{0:T(128)S(1)}, s32[4]{0:T(128)}, u32[]{:S(2)}) copy-start(s32[4]{0:T(128)} %param.19) | copy-start | bytes 52
  55.5 9.3 %copy-start.5 = (s32[4,2]{0,1:T(2,128)S(1)}, s32[4,2]{0,1:T(2,128)}, u32[]{:S(2)}) copy-start(s32[4,2]{0,1:T(2,128)} %param.20) | copy-start | bytes 100
  59.0 21.4 %all-to-all-start = ((bf16[8,4,512]{2,1,0:T(4,128)(2,1)}), bf16[8,4,512]{2,1,0:T(4,128)(2,1)S(1)}, u32[]{:S(2)}, u32[]{:S(2)}) async-start(bf16[8,4,512]{2,1,0:T(4,128)(2,1)} %broadcast_in_dim.28), calls=%async_computation | async-start | bytes 65536 | tf_op jit(solution)/shard_map/all_to_all | solution.py:182
  71.9 7.0 %slice-start = ((bf16[6,8,8,2,7,4,128]{6,5,4,3,2,1,0:T(4,128)(2,1)}), bf16[2,8,8,2,7,4,128]{6,5,4,3,2,1,0:T(4,128)(2,1)S(1)}, s32[]{:S(2)}) async-start(bf16[6,8,8,2,7,4,128]{6,5,4,3,2,1,0:T(4,128)(2,1)} %copy-done), calls=%async_computation.2 | async-start | bytes 3670016 | tf_op jit(solution)/shard_map/slice | solution.py:337
  71.9 8.8 %copy-start.4 = (f32[64]{0:T(128)S(1)}, f32[64]{0:T(128)}, u32[]{:S(2)}) copy-start(f32[64]{0:T(128)} %constant.64.clone) | copy-start | bytes 772
  84.8 36.6 %copy-start.1 = (bf16[2,448,8,128]{3,2,0,1:T(8,128)(2,1)S(1)}, bf16[2,448,8,128]{3,2,0,1:T(8,128)(2,1)}, u32[]{:S(2)}) copy-start(bf16[2,448,8,128]{3,2,0,1:T(8,128)(2,1)} %copy.408) | copy-start | bytes 5505028
  122.8 12.7 %all-to-all-start.1 = ((f32[8,4,3584]{2,1,0:T(4,128)}), f32[8,4,3584]{2,1,0:T(4,128)S(1)}, u32[]{:S(2)}, u32[]{:S(2)}) async-start(f32[8,4,3584]{2,1,0:T(4,128)} %broadcast_in_dim.35), calls=%async_computation.1 | async-start | bytes 917504 | tf_op jit(solution)/shard_map/all_to_all | solution.py:182

commit v2 on v0

v2 whole, which is shorter than its diff:
```python
import jax
import jax.numpy as jnp
import numpy as np
from jax import lax
from jax.experimental import pallas as pl
from jax.experimental.pallas import tpu as pltpu
from jax.sharding import Mesh
from jax.sharding import PartitionSpec as P

HQ = 16
KVH = 4
HD = 128
BLOCK = 512
STRETCH = 8192
ROWS = 28
GROUPS = 7
HERE = 1024
TP = ("tp_0", "tp_1")
SEQ = ("seq_0", "seq_1")
SEQ_TP = ("seq_0", "seq_1", "tp_0", "tp_1")
SEQ_TP_ROLL = ("seq_0", "seq_1", "tp_0", "tp_1", "roll")
MESH = pl.DeviceIdType.MESH
F32 = jnp.float32
BF16 = jnp.bfloat16

rope_base = 10000000.0
norm_eps = 1e-06
lowest = -1e30
floor_top = -1e20


def frequencies(width):
    half_width = width // 2
    exact = rope_base ** (-2.0 * np.arange(half_width) / width)
    octave = np.floor(np.log2(exact))
    quantum = 2.0 ** (8.0 - octave)
    return np.floor(exact * quantum) / quantum


def normalize(row_block, norm_gain):
    wide_rows = row_block.astype(F32)
    scaled = wide_rows * lax.rsqrt(
        jnp.mean(wide_rows * wide_rows, axis=1, keepdims=True) + norm_eps
    )
    return (scaled * norm_gain.astype(F32)).astype(BF16)


def device(x, y, z, core):
    return (x % 2, z, y, core, x // 2)


ORDER = (0, -1, 1, 2)
TP_STEPS = tuple((dy, dc) for dy in (0, 3, 1, 2) for dc in (0, 1))
PLANE_STEPS = tuple((dx, dz) for dx in (2, 1, 3, 0) for dz in (2, 1, 3, 0))


def layer_kernel(
    tiles_ref, normed_ref, bias_ref, turn_ref, len_ref, key_ref, value_ref,
    w_ref, fresh_ref, final_ref,
    kbuf, vbuf, other, wq, part, r2, qb, rot, self_s, s_buf, p_buf, ob, r5, c6, r6, po, r7,
    cache_sem, own_sem, trade_send, trade_recv, ring_send, ring_recv, pair_sem, other_sem,
    stage_send, recv2, recv3, recv5, recv6, recv7, recv8,
):
    x = lax.axis_index("roll") * 2 + lax.axis_index("seq_0")
    y, z, core = lax.axis_index("tp_0"), lax.axis_index("seq_1"), lax.axis_index("tp_1")
    seq, roll, tp = (x % 2) * 4 + z, x // 2, y * 2 + core

    def remote(src, dst, send, recv, target):
        return pltpu.make_async_remote_copy(
            src_ref=src, dst_ref=dst, send_sem=send, recv_sem=recv,
            device_id=device(*target), device_id_type=MESH,
        )

    def tp_peer(dy, dc):
        return (x, (y + dy) % 4, z, (core + dc) % 2)

    def plane_peer(dx, dz):
        return ((x + dx) % 4, y, (z + dz) % 4, core)

    partners = [tp_peer(dy, dc) for dy, dc in TP_STEPS if (dy, dc) != (0, 0)]
    partners += [plane_peer(dx, dz) for dx, dz in PLANE_STEPS if (dx, dz) != (0, 0)]

    caches = []
    for r in range(4):
        caches.append(pltpu.make_async_copy(key_ref.at[r], kbuf.at[r], cache_sem.at[0, r]))
    for r in range(4):
        caches.append(pltpu.make_async_copy(value_ref.at[r], vbuf.at[r], cache_sem.at[1, r]))

    barrier = pltpu.get_barrier_semaphore()
    for partner in partners:
        pl.semaphore_signal(barrier, inc=1, device_id=device(*partner), device_id_type=MESH)

    def tiles_of(kind, ty, tcore):
        t = ty * 2 + tcore
        return (24 + 2 * t, 2) if kind == 0 else (2 * t, 2) if kind == 1 else (16 + 4 * tcore + ty, 1)

    def place_of(kind, tcore):
        return (0, 2) if kind == 0 else (2, 2) if kind == 1 else (4 + tcore, 1)

    def traded(kind, dy, dc):
        ty, tcore = (y + dy) % 4, (core + dc) % 2
        first, count = tiles_of(kind, ty, tcore)
        to, _ = place_of(kind, tcore)
        src = tiles_ref.at[pl.ds(first, count)]
        dst = w_ref.at[pl.ds(to, count), seq, tp, roll]
        if (dy, dc) == (0, 0):
            return pltpu.make_async_copy(src, dst, own_sem.at[kind])
        return remote(src, dst, trade_send.at[kind], trade_recv.at[kind, dy * 2 + dc], (x, ty, z, tcore))

    def got_trade(kind):
        to, count = place_of(kind, core)
        for dy, dc in TP_STEPS:
            if (dy, dc) == (0, 0):
                traded(kind, 0, 0).wait()
            else:
                source = ((y - dy) % 4) * 2 + (core + dc) % 2
                here = w_ref.at[pl.ds(to, count), seq, source, roll]
                remote(here, here, trade_send.at[kind], trade_recv.at[kind, dy * 2 + dc], tp_peer(dy, dc)).wait_recv()

    for kind in range(3):
        traded(kind, 0, 0).start()
    pl.semaphore_wait(barrier, len(partners))

    across = remote(normed_ref.at[1], other, other_sem.at[0], other_sem.at[1], plane_peer(2, 0))
    across.start()
    for kind in range(3):
        for dy, dc in TP_STEPS:
            if (dy, dc) != (0, 0):
                traded(kind, dy, dc).start()
    for copy in caches:
        copy.start()

    def region(kind, half):
        if kind < 2:
            return kind * 2 + half, 0, 8
        return 4 + core, half * 4, 4

    def block_at(kind, half, bx, bz, part_of):
        tile, first, count = region(kind, half)
        if part_of is not None:
            count = count // 2
            first = first + part_of * count
        return w_ref.at[pl.ds(tile, 1), (bx % 2) * 4 + bz, pl.ds(first, count), bx // 2]

    def coords(half, f, g):
        return ((x + g) % 4, (z + f) % 4) if half == 0 else ((x + f) % 4, (z + g) % 4)

    def ring(kind, half, message, f, g, part_of, step):
        bx, bz = coords(half, f, g)
        tx, tz = coords(half, *step)
        block = block_at(kind, half, bx, bz, part_of)
        return remote(block, block, ring_send.at[kind], ring_recv.at[kind, half * 20 + message], (tx, y, tz, core))

    def to_pair(kind, half, f, g, part_of=None):
        if kind == 2:
            bx, bz = coords(half, f, g)
            block = block_at(kind, half, bx, bz, part_of)
            remote(block, block, pair_sem.at[0], pair_sem.at[1], tp_peer(0, 1)).start()

    def sideways(kind, half, f):
        k = 4 + ORDER.index(f) * 4
        ring(kind, half, k, f, 0, None, (0, 1)).start()
        ring(kind, half, k + 1, f, 0, None, (0, -1)).start()

    def s1(kind):
        for half in (0, 1):
            ring(kind, half, 0, 0, 0, None, (1, 0)).start()
            ring(kind, half, 1, 0, 0, None, (-1, 0)).start()
        for half in (0, 1):
            sideways(kind, half, 0)
            to_pair(kind, half, 0, 0)

    def s2(kind):
        for half in (0, 1):
            ring(kind, half, 0, -1, 0, None, (1, 0)).wait_recv()
            ring(kind, half, 2, -1, 0, 0, (1, 0)).start()
            ring(kind, half, 1, 1, 0, None, (1, 0)).wait_recv()
            ring(kind, half, 3, 1, 0, 1, (-1, 0)).start()
        for half in (0, 1):
            for f in (-1, 1):
                sideways(kind, half, f)
                to_pair(kind, half, f, 0)

    def s3(kind):
        for half in (0, 1):
            ring(kind, half, 2, 2, 0, 0, (1, 0)).wait_recv()
            ring(kind, half, 3, 2, 0, 1, (1, 0)).wait_recv()
            sideways(kind, half, 2)
            to_pair(kind, half, 2, 0)

    def s4(kind, fs=ORDER):
        for f in fs:
            for half in (0, 1):
                k = 4 + ORDER.index(f) * 4
                ring(kind, half, k, f, -1, None, (0, 1)).wait_recv()
                ring(kind, half, k + 2, f, -1, 0, (0, 1)).start()
                to_pair(kind, half, f, -1)
                ring(kind, half, k + 1, f, 1, None, (0, 1)).wait_recv()
                ring(kind, half, k + 3, f, 1, 1, (0, -1)).start()
                to_pair(kind, half, f, 1)

    def s5(kind):
        for f in ORDER:
            for half in (0, 1):
                k = 4 + ORDER.index(f) * 4
                ring(kind, half, k + 2, f, 2, 0, (0, 1)).wait_recv()
                to_pair(kind, half, f, 2, 0)
                ring(kind, half, k + 3, f, 2, 1, (0, 1)).wait_recv()
                to_pair(kind, half, f, 2, 1)
        sent = w_ref.at[0:5, 0 : (6 if kind < 2 else 3), :, 0]
        remote(sent, sent, ring_send.at[kind], ring_recv.at[kind, 0], plane_peer(0, 1)).wait_send()

    def tp_send(stage, src_of, dst, sems):
        for dy, dc in TP_STEPS:
            if (dy, dc) != (0, 0):
                target = tp_peer(dy, dc)
                remote(src_of(target[1] * 2 + target[3]), dst, stage_send.at[stage], sems.at[dy * 2 + dc], target).start()

    def tp_wait(stage, buffer, sems):
        for dy, dc in TP_STEPS:
            if (dy, dc) != (0, 0):
                here = buffer.at[((y - dy) % 4) * 2 + (core + dc) % 2]
                remote(here, here, stage_send.at[stage], sems.at[dy * 2 + dc], tp_peer(dy, dc)).wait_recv()

    def sent_all(stage, buffer, count):
        sent = buffer.at[0:count]
        remote(sent, sent, stage_send.at[stage], recv3.at[0], tp_peer(0, 1)).wait_send()

    def project():
        got_trade(1)
        got_trade(2)
        across.wait_recv()
        for k in range(3):
            tile = (2 + k) if k < 2 else 4 + core
            rows = w_ref[tile, seq, :, roll]
            wq[:, k * HD : (k + 1) * HD] = rows.reshape(8 * ROWS, HD)
        for k, lhs in ((0, normed_ref[0]), (1, other[...])):
            made = jnp.dot(lhs, wq[...], preferred_element_type=F32)
            part[k] = made[0:4]
        r2[x * 4 + z] = part[0]
        for dx, dz in PLANE_STEPS:
            if (dx, dz) != (0, 0):
                tx, _, tz, _ = plane_peer(dx, dz)
                remote(
                    part.at[(tx // 2 + roll) % 2], r2.at[x * 4 + z], stage_send.at[0],
                    recv2.at[dx * 4 + dz], (tx, y, tz, core),
                ).start()

    def share():
        for dx, dz in PLANE_STEPS:
            if (dx, dz) != (0, 0):
                here = r2.at[((x - dx) % 4) * 4 + (z - dz) % 4]
                remote(here, here, stage_send.at[0], recv2.at[dx * 4 + dz], plane_peer(dx, dz)).wait_recv()
        total = r2[0]
        for k in range(1, 16):
            total = total + r2[k]
        for k in range(3):
            row = (2 * tp + k) if k < 2 else 16 + 4 * core + y
            qb[tp, k] = (total[:, k * HD : (k + 1) * HD] + bias_ref[row]).astype(BF16)
        tp_send(1, lambda t: qb.at[tp], qb.at[tp], recv3)

    def turn(v, position):
        return v * turn_ref[position, 0] + pltpu.roll(v, 64, v.ndim - 1) * turn_ref[position, 1]

    def queries():
        tp_wait(1, qb, recv3)
        for g in range(KVH):
            fresh_key = turn(qb[2 * g, 2].astype(F32), 0).astype(BF16)
            fresh_ref[:, g * HD : (g + 1) * HD] = fresh_key
            fresh_ref[:, (KVH + g) * HD : (KVH + g + 1) * HD] = qb[2 * g + 1, 2]
            for h in range(4 * g, 4 * g + 4):
                q = qb[h // 2, h % 2].astype(F32)
                own = turn(q, 0).astype(BF16).astype(F32)
                score = jnp.sum(own * fresh_key.astype(F32), axis=1, keepdims=True) * HD ** (-0.5)
                self_s[4 * h : 4 * h + 4] = jnp.broadcast_to(score, (4, HD))
                for b in range(2):
                    rot[b, 4 * h : 4 * h + 4] = turn(q, 1 + b)

    def scores():
        start = (seq * 8 + tp) * HERE
        owner = lax.broadcasted_iota(jnp.int32, (16, BLOCK), 0) % 4
        column = lax.broadcasted_iota(jnp.int32, (16, BLOCK), 1)
        for r in range(4):
            caches[r].wait()
            for b in range(2):
                valid = (owner == r) & (column + (start + b * BLOCK) < len_ref[r])
                for g in range(KVH):
                    rows, cols = slice(16 * g, 16 * g + 16), slice(b * BLOCK, (b + 1) * BLOCK)
                    made = lax.dot_general(
                        rot[b, rows].astype(BF16), kbuf[r, cols, g * HD : (g + 1) * HD],
                        (((1,), (1,)), ((), ())), preferred_element_type=F32,
                    )
                    before = s_buf[rows, cols] if r > 0 else jnp.full((16, BLOCK), lowest, F32)
                    s_buf[rows, cols] = jnp.where(valid, made * HD ** (-0.5), before)

    def values():
        for g in range(KVH):
            s = s_buf[16 * g : 16 * g + 16]
            top = jnp.maximum(jnp.max(s, axis=1, keepdims=True), floor_top)
            w = jnp.exp(s - top)
            p_buf[16 * g : 16 * g + 16] = w.astype(BF16)
            low = jnp.sum(w, axis=1, keepdims=True)
            for k in range(2):
                rows = slice(8 * k, 8 * k + 8)
                ob[2 * g + k, 0] = jnp.broadcast_to(top[rows], (8, HD))
                ob[2 * g + k, 1] = jnp.broadcast_to(low[rows], (8, HD))
        owner = lax.broadcasted_iota(jnp.int32, (16, HERE), 0) % 4
        for r in range(4):
            caches[4 + r].wait()
        for g in range(KVH):
            total = jnp.zeros((16, HD), F32)
            w = p_buf[16 * g : 16 * g + 16].astype(F32)
            for r in range(4):
                mine = jnp.where(owner == r, w, 0.0).astype(BF16)
                total += jnp.dot(mine, vbuf[r, :, g * HD : (g + 1) * HD], preferred_element_type=F32)
            ob[2 * g, 2] = total[0:8]
            ob[2 * g + 1, 2] = total[8:16]
        r5[tp] = ob[tp]
        tp_send(2, lambda t: ob.at[t], r5.at[tp], recv5)

    def combined(buffer):
        top = buffer[0, 0]
        for k in range(1, 8):
            top = jnp.maximum(top, buffer[k, 0])
        low, out = jnp.zeros_like(top), jnp.zeros_like(top)
        for k in range(8):
            factor = jnp.exp(buffer[k, 0] - top)
            low += buffer[k, 1] * factor
            out += buffer[k, 2] * factor
        return top, low, out

    def over_tp():
        tp_wait(2, r5, recv5)
        for k, value in enumerate(combined(r5)):
            c6[k] = value
            r6[seq, k] = value
        for dl in range(2):
            for dz in (2, 1, 3, 0):
                if dl + dz > 0:
                    tx, tz = roll * 2 + (x + dl) % 2, (z + dz) % 4
                    remote(c6, r6.at[seq], stage_send.at[3], recv6.at[dl * 4 + dz], (tx, y, tz, core)).start()

    def finish():
        for dl in range(2):
            for dz in (2, 1, 3, 0):
                if dl + dz > 0:
                    here = r6.at[((x + dl) % 2) * 4 + (z - dz) % 4]
                    remote(here, here, stage_send.at[3], recv6.at[dl * 4 + dz], plane_peer(0, 1)).wait_recv()
        old_top, old_low, old_out = combined(r6)
        mine = self_s[pl.ds(pl.multiple_of(tp * 8, 8), 8)]
        top = jnp.maximum(old_top, mine)
        factor, fresh = jnp.exp(old_top - top), jnp.exp(mine - top)
        own_value = qb[(tp // 2) * 2 + 1, 2].astype(F32)
        both = jnp.concatenate([own_value, own_value], axis=0)
        numerator = old_out * factor + fresh.astype(BF16).astype(F32) * both
        attention = (numerator / (old_low * factor + fresh)).astype(BF16)
        return attention

    def out_project(attention):
        for o in range(8):
            sums = []
            for k in range(2):
                rows = w_ref[k, o].reshape(16 * ROWS, HD)
                sums.append(lax.dot_general(attention, rows, (((1,), (1,)), ((), ())), preferred_element_type=F32))
            po[o, :, 0:448] = sums[0][0:4] + sums[1][4:8]
            po[o, :, 448:512] = jnp.zeros((4, 64), F32)
        r7[tp] = po[tp]
        tp_send(4, lambda t: po.at[t], r7.at[tp], recv7)

    def reduce_out():
        tp_wait(4, r7, recv7)
        total = r7[0]
        for k in range(1, 8):
            total = total + r7[k]
        final_ref[tp] = total.astype(BF16)
        tp_send(5, lambda t: final_ref.at[tp], final_ref.at[tp], recv8)

    got_trade(0)
    s1(0)
    project()
    s1(1)
    s2(0)
    share()
    s3(0)
    s1(2)
    queries()
    s2(1)
    scores()
    s4(0)
    values()
    s3(1)
    s2(2)
    over_tp()
    s5(0)
    s4(1)
    out_project(finish())
    s3(2)
    s4(2)
    reduce_out()
    s5(1)
    s5(2)
    tile = w_ref.at[5 - core]
    whole = remote(tile, tile, pair_sem.at[0], pair_sem.at[1], tp_peer(0, 1))
    whole.wait_send()
    whole.wait_recv()
    tp_wait(5, final_ref, recv8)
    for kind in range(3):
        sent = tiles_ref.at[0 : (14 if kind < 2 else 7)]
        remote(sent, sent, trade_send.at[kind], trade_recv.at[kind, 1], tp_peer(0, 1)).wait_send()
    across.wait_send()
    sent_all(0, r2, 15)
    sent_all(1, qb, 7)
    sent_all(2, ob, 7)
    sent_all(3, r6, 7)
    sent_all(4, po, 7)
    sent_all(5, final_ref, 7)


def layer(tiles, normed, bias, turns, lengths, keys, values):
    hbm, vmem = pl.BlockSpec(memory_space=pltpu.HBM), pl.BlockSpec(memory_space=pltpu.VMEM)
    smem, dma = pl.BlockSpec(memory_space=pltpu.SMEM), pltpu.SemaphoreType.DMA
    return pl.pallas_call(
        layer_kernel,
        name="layer",
        out_shape=(
            jax.ShapeDtypeStruct((6, 8, 8, 2, GROUPS, 4, HD), BF16),
            jax.ShapeDtypeStruct((4, 2 * KVH * HD), BF16),
            jax.ShapeDtypeStruct((8, 4, 512), BF16),
        ),
        in_specs=[hbm, vmem, vmem, vmem, smem, hbm, hbm],
        out_specs=(vmem, vmem, vmem),
        scratch_shapes=[
            pltpu.VMEM((4, HERE, KVH * HD), BF16),
            pltpu.VMEM((4, HERE, KVH * HD), BF16),
            pltpu.VMEM((8, 8 * ROWS), BF16),
            pltpu.VMEM((8 * ROWS, 3 * HD), BF16),
            pltpu.VMEM((2, 4, 3 * HD), F32),
            pltpu.VMEM((16, 4, 3 * HD), F32),
            pltpu.VMEM((8, 3, 4, HD), BF16),
            pltpu.VMEM((2, 64, HD), F32),
            pltpu.VMEM((64, HD), F32),
            pltpu.VMEM((64, HERE), F32),
            pltpu.VMEM((64, HERE), BF16),
            pltpu.VMEM((8, 3, 8, HD), F32),
            pltpu.VMEM((8, 3, 8, HD), F32),
            pltpu.VMEM((3, 8, HD), F32),
            pltpu.VMEM((8, 3, 8, HD), F32),
            pltpu.VMEM((8, 4, 512), F32),
            pltpu.VMEM((8, 4, 512), F32),
            dma((2, 4)), dma((3,)), dma((3,)), dma((3, 8)), dma((3,)), dma((3, 40)), dma((2,)), dma((2,)),
            dma((6,)), dma((16,)), dma((8,)), dma((8,)), dma((8,)), dma((8,)), dma((8,)),
        ],
        compiler_params=pltpu.CompilerParams(collective_id=0, has_side_effects=True, vmem_limit_bytes=36 * 2**20),
    )(tiles, normed, bias, turns, lengths, keys, values)


def body(
    hidden,
    norm_gain,
    qkv_bias,
    qkv_weight,
    out_weight,
    key_cache,
    value_cache,
    cache_len,
    block_pos,
):
    rollouts = hidden.shape[0]
    rows = jnp.concatenate([qkv_weight, out_weight], axis=1).reshape(ROWS, 40, HD)
    tiles = jnp.transpose(rows, (1, 0, 2)).reshape(40, GROUPS, 4, HD)
    normed = normalize(hidden, norm_gain)
    near = lax.dynamic_slice_in_dim(normed, lax.axis_index(SEQ) * 448, 448, 1)
    near = near.reshape(rollouts, 8, 2, ROWS)
    odd = lax.axis_index("roll") == 1
    even_rows, odd_rows = (near[:, :, k].reshape(rollouts, 8 * ROWS) for k in (0, 1))
    chosen = jnp.stack([jnp.where(odd, odd_rows, even_rows), jnp.where(odd, even_rows, odd_rows)])
    chosen = jnp.pad(chosen, ((0, 0), (0, 4), (0, 0)))
    bias = qkv_bias.astype(F32).reshape(24, 1, HD)
    inverse = jnp.asarray(frequencies(HD), dtype=F32)
    positions = jnp.concatenate([(cache_len % STRETCH)[:, None], block_pos], axis=1)
    angles = positions.T.astype(F32)[..., None] * inverse
    cosine, sine = jnp.cos(angles), jnp.sin(angles)
    turns = jnp.stack(
        [jnp.concatenate([cosine, cosine], axis=-1), jnp.concatenate([-sine, sine], axis=-1)], axis=1
    )
    w, fresh_kv, final = layer(tiles, chosen, bias, turns, cache_len, key_cache, value_cache)
    joint = w.reshape(6, 3584, HD)
    served_out = jnp.moveaxis(joint[:2], 0, 1).reshape(3584, 2 * HD)
    served_qkv = jnp.moveaxis(joint[2:], 0, 1).reshape(3584, 4 * HD)
    attended = jnp.moveaxis(final[:, :, :448], 0, 1).reshape(rollouts, 3584)
    return (attended, fresh_kv, served_qkv, served_out)


def solution(mesh):
    finer = Mesh(
        mesh.devices.reshape(2, 4, 4, 2, mesh.shape["roll"]),
        ("seq_0", "seq_1", "tp_0", "tp_1", "roll"),
    )
    in_specs = (
        P("roll", None),
        P(),
        P(),
        P(SEQ_TP_ROLL, None),
        P(SEQ_TP_ROLL, None),
        P("roll", SEQ_TP, None),
        P("roll", SEQ_TP, None),
        P("roll"),
        P("roll", SEQ_TP),
    )
    out_specs = (P("roll", None), P("roll", None), P(None, TP), P(None, TP))
    return jax.shard_map(body, mesh=finer, in_specs=in_specs, out_specs=out_specs, check_vma=False)
```

time: 195 us -> 76.1 us (0.39)
  waiting for transfers between devices: 70.7 us -> 0 us
  blocking collectives: 63 us -> 0 us
  Pallas kernels: 0 us -> 49.1 us
  between operations: 14.6 us -> 0.74 us
  starting transfers between devices: 9.16 us -> 0 us
  matrix products: 8.1 us -> 0 us
  local copies, waits for them, and re-layouts: 23.1 us -> 19.9 us
    all_gather x1 -> x0, waiting for transfers between devices: 62.7 us -> none  [side_by_side_3(): whole, at, outs = (lax.all_gather(both, axis, axis=dim, tiled=True), 0, [])]
    pallas_call x0 -> x1, Pallas kernels: none -> 49.1 us  [layer(): pl.pallas_call(layer_kernel, name='layer', out_shape=(jax.ShapeDtypeStruc...]
    all_to_all x2 -> x0, blocking collectives: 31.9 us -> none  [the longest x1 17.3 us: side_by_side_2(): lax.all_to_all(both, axis, split_axis=split_dim, concat_axis=concat_dim,...]
    all_gather x4 -> x0, blocking collectives: 31.1 us -> none  [gathered_once(): both, at, found = (lax.all_gather(jnp.concatenate(lines), axis), 0, {})]
    reshape x18 -> x6, local copies, waits for them, and re-layouts: 14.3 us -> 4.97 us  [the longest x1 2.47 us: body(): served_qkv = jnp.moveaxis(joint[2:], 0, 1).reshape(3584, 4 * HD)]
    all_to_all x2 -> x0, starting transfers between devices: 9.13 us -> none  [from_everyone(): return lax.all_to_all(copies, axis, split_axis=0, concat_axis=0, tiled=True)]
    dot_general x5 -> x0, matrix products: 8.1 us -> none  [the longest x1 3.7 us: body(): jnp.einsum('rbkgd,rbpkd->rkgbp', block_query.reshape(rollouts, blocks, KV...]
    all_to_all x2 -> x0, waiting for transfers between devices: 7.95 us -> none  [from_everyone(): return lax.all_to_all(copies, axis, split_axis=0, concat_axis=0, tiled=True)]
  transfers between devices with their start and end apart: 3 -> 0, of which waited for: 2 -> 0; matrix products, arithmetic and copies ran while one was open for 9% -> 0% of each run, Pallas kernels for 0% -> 0%
where the time goes in v2:
time: 76.1 us; the launch traced here: 75.6 us
  Pallas kernels  49.1 us (65%)
  local copies, waits for them, and re-layouts  19.9 us (26%)
  other arithmetic  5.8 us (8%)
    pallas_call x1, Pallas kernels, layer(): pl.pallas_call(layer_kernel, name='layer', out_shape=(jax.ShapeDtypeStruc...  49.1 us
    unnamed x10, local copies, waits for them, and re-layouts  8.05 us
    slice x1, local copies, waits for them, and re-layouts, body(): served_qkv = jnp.moveaxis(joint[2:], 0, 1).reshape(3584, 4 * HD)  3.76 us
    reshape x1, local copies, waits for them, and re-layouts, body(): served_qkv = jnp.moveaxis(joint[2:], 0, 1).reshape(3584, 4 * HD)  2.47 us
    slice x1, local copies, waits for them, and re-layouts, body(): served_out = jnp.moveaxis(joint[:2], 0, 1).reshape(3584, 2 * HD)  2.17 us
    reshape x1, local copies, waits for them, and re-layouts, body(): served_out = jnp.moveaxis(joint[:2], 0, 1).reshape(3584, 2 * HD)  1.54 us

profile of v2, /device:TPU:1, one launch (start us, length us, event | category | flops | bytes accessed | tf_op | source)
XLA Modules:
  0.0 75.6 jit_solution(16300377818331836566)
XLA Ops:
  0.6 0.9 %multiply_reduce_fusion = f32[4]{0:T(128)S(1)} fusion(bf16[4,3584]{1,0:T(4,128)(2,1)} %param.10), kind=kLoop, calls=%fused_computation.3 | loop fusion | flops 43004 | bytes 28688 | tf_op jit(solution)/shard_map/reduce_sum | solution.py:43
  1.5 0.7 fusion.8
  2.2 0.7 fusion.7
  2.9 0.8 %dynamic-slice = f32[448]{0:T(512)S(1)} dynamic-slice(bf16[3584]{0:T(1024)(128)(2,1)} %param.11, s32[]{:T(128)S(6)} %select_n.43), dynamic_slice_sizes={448} | dynamic-slice | bytes 3588 | tf_op jit(solution)/shard_map/dynamic_slice | solution.py:472
  3.7 0.7 reshape.91
  4.4 0.8 %multiply_cosine_fusion = (f32[3,4,64]{2,1,0:T(4,128)S(1)}, f32[3,4,64]{2,1,0:T(4,128)S(1)}, f32[3,4,64]{2,1,0:T(4,128)S(1)}) fusion(f32[64]{0:T(128)} %constant.49.clone, f32[3,4]{1,0:T(4,128)S(1)} %fusion.7), kind=kLoop, calls=%fused_computation.14 | loop fusion | flops 1536 | bytes 9520 | tf_op jit(solution)/shard_map/cos | solution.py:482
  5.1 0.1 maximum_bitcast_fusion
  5.2 0.8 %convert_element_type.18 = f32[4,3584]{1,0:T(4,128)S(1)} convert(bf16[4,3584]{1,0:T(4,128)(2,1)} %param.10) | non-fusion elementwise | flops 14336 | bytes 86016 | tf_op jit(solution)/shard_map/convert_element_type | solution.py:41
  6.0 0.1 fusion.6
  6.1 0.1 reshape.85
  6.2 0.1 fusion
  6.3 0.1 select_n.45
  6.4 0.1 select_n.47
  6.5 1.0 %pad_maximum_fusion = bf16[28,5120]{1,0:T(8,128)(2,1)S(1)} fusion(bf16[28,2048]{1,0:T(8,128)(2,1)} %param.14, bf16[28,3072]{1,0:T(8,128)(2,1)} %param.13), kind=kLoop, calls=%fused_computation.2 | loop fusion | flops 573440 | bytes 573440 | tf_op jit(solution)/shard_map/concatenate | solution.py:469
  7.6 0.1 copy.24.tiles_ref
  7.7 0.0 copy-start.1
  7.7 2.2 %copy-done.1 = bf16[4,1024,512]{2,1,0:T(8,128)(2,1)S(1)} copy-done((bf16[4,1024,512]{2,1,0:T(8,128)(2,1)S(1)}, bf16[4,1024,512]{2,1,0:T(8,128)(2,1)}, u32[]{:S(2)}) %copy-start.1) | copy-done | bytes 4194328
  9.9 0.0 copy-start.2
  9.9 2.2 %copy-done.2 = bf16[4,1024,512]{2,1,0:T(8,128)(2,1)S(1)} copy-done((bf16[4,1024,512]{2,1,0:T(8,128)(2,1)S(1)}, bf16[4,1024,512]{2,1,0:T(8,128)(2,1)}, u32[]{:S(2)}) %copy-start.2) | copy-done | bytes 4194328
  12.1 0.0 copy-start.3
  12.1 0.7 copy-done.3
  12.7 49.1 %layer.1 = (bf16[6,8,8,2,7,4,128]{6,5,4,3,2,1,0:T(4,128)(2,1)S(1)}, bf16[4,1024]{1,0:T(4,128)(2,1)S(1)}, bf16[8,4,512]{2,1,0:T(4,128)(2,1)S(1)}) custom-call(bf16[40,7,4,128]{3,2,1,0:T(4,128)(2,1)S(1)} %copy.24.tiles_ref, bf16[2,8,224]{2,1,0:T(8,128)(2,1)S(1)} %fusion.4.normed_ref, f32[24,1,128]{2,1,0:T(1,128)S(1)} %bitcast.33, ...), custom_call_target="tpu_custom_call" | custom-call | tf_op jit(solution)/shard_map/layer/pallas_call | solution.py:422
  61.9 0.0 copy-start
  61.9 2.4 %copy-done = bf16[6,8,8,2,7,4,128]{6,5,4,3,2,1,0:T(4,128)(2,1)} copy-done((bf16[6,8,8,2,7,4,128]{6,5,4,3,2,1,0:T(4,128)(2,1)}, bf16[6,8,8,2,7,4,128]{6,5,4,3,2,1,0:T(4,128)(2,1)S(1)}, u32[]{:S(2)}) %copy-start) | copy-done | bytes 5505048
  64.3 0.7 reshape.88
  65.0 2.2 %slice.26 = bf16[2,8,8,2,7,4,128]{6,5,4,3,2,1,0:T(4,128)(2,1)S(1)} slice(bf16[6,8,8,2,7,4,128]{6,5,4,3,2,1,0:T(4,128)(2,1)} %copy-done), slice={[0:2], [0:8], [0:8], [0:2], [0:7], [0:4], [0:128]} | slice | bytes 3670016 | tf_op jit(solution)/shard_map/slice | solution.py:488
  67.2 3.8 %slice.24 = bf16[4,8,8,2,7,4,128]{6,5,4,3,2,1,0:T(4,128)(2,1)S(1)} slice(bf16[6,8,8,2,7,4,128]{6,5,4,3,2,1,0:T(4,128)(2,1)} %copy-done), slice={[2:6], [0:8], [0:8], [0:2], [0:7], [0:4], [0:128]} | slice | bytes 7340032 | tf_op jit(solution)/shard_map/slice | solution.py:489
  70.9 2.5 %copy.33 = bf16[4,448,8,128]{3,2,0,1:T(8,128)(2,1)} copy(bf16[4,448,8,128]{3,2,1,0:T(8,128)(2,1)S(1)} %bitcast.34) | data formatting | bytes 7340032 | tf_op jit(solution)/shard_map/reshape | solution.py:489
  73.4 1.5 %copy.34 = bf16[2,448,8,128]{3,2,0,1:T(8,128)(2,1)} copy(bf16[2,448,8,128]{3,2,1,0:T(8,128)(2,1)S(1)} %bitcast.35) | data formatting | bytes 3670016 | tf_op jit(solution)/shard_map/reshape | solution.py:488
  75.0 0.6 copy.36
  (7 shorter events, 0.1 us)
Async XLA Ops:
  7.7 2.2 %copy-start.1 = (bf16[4,1024,512]{2,1,0:T(8,128)(2,1)S(1)}, bf16[4,1024,512]{2,1,0:T(8,128)(2,1)}, u32[]{:S(2)}) copy-start(bf16[4,1024,512]{2,1,0:T(8,128)(2,1)} %key_ref.1) | copy-start | bytes 12582916
  9.9 2.2 %copy-start.2 = (bf16[4,1024,512]{2,1,0:T(8,128)(2,1)S(1)}, bf16[4,1024,512]{2,1,0:T(8,128)(2,1)}, u32[]{:S(2)}) copy-start(bf16[4,1024,512]{2,1,0:T(8,128)(2,1)} %value_ref.1) | copy-start | bytes 12582916
  12.1 0.7 copy-start.3
  61.9 2.4 %copy-start = (bf16[6,8,8,2,7,4,128]{6,5,4,3,2,1,0:T(4,128)(2,1)}, bf16[6,8,8,2,7,4,128]{6,5,4,3,2,1,0:T(4,128)(2,1)S(1)}, u32[]{:S(2)}) copy-start(bf16[6,8,8,2,7,4,128]{6,5,4,3,2,1,0:T(4,128)(2,1)S(1)} %get-tuple-element.9) | copy-start | bytes 16515076

commit v3 on v2

--- a/solution.py
+++ b/solution.py
@@ -37,14 +37,6 @@
     return np.floor(exact * quantum) / quantum
 
 
-def normalize(row_block, norm_gain):
-    wide_rows = row_block.astype(F32)
-    scaled = wide_rows * lax.rsqrt(
-        jnp.mean(wide_rows * wide_rows, axis=1, keepdims=True) + norm_eps
-    )
-    return (scaled * norm_gain.astype(F32)).astype(BF16)
-
-
 def device(x, y, z, core):
     return (x % 2, z, y, core, x // 2)
 
@@ -55,10 +47,11 @@
 
 
 def layer_kernel(
-    tiles_ref, normed_ref, bias_ref, turn_ref, len_ref, key_ref, value_ref,
+    hidden_ref, gain_ref, bias_hbm, qkv_ref, out_ref, len_ref, pos_ref, key_ref, value_ref,
     w_ref, fresh_ref, final_ref,
-    kbuf, vbuf, other, wq, part, r2, qb, rot, self_s, s_buf, p_buf, ob, r5, c6, r6, po, r7,
-    cache_sem, own_sem, trade_send, trade_recv, ring_send, ring_recv, pair_sem, other_sem,
+    hidden_in, gain_in, bias_in, qkv_in, out_in, tiles_ref, near, bias_ref, turn_ref,
+    kbuf, vbuf, normed_ref, other, wq, part, r2, qb, rot, self_s, s_buf, p_buf, ob, r5, c6, r6, po, r7,
+    load_sem, cache_sem, trade_send, trade_recv, ring_send, ring_recv, pair_sem, other_sem,
     stage_send, recv2, recv3, recv5, recv6, recv7, recv8,
 ):
     x = lax.axis_index("roll") * 2 + lax.axis_index("seq_0")
@@ -89,6 +82,49 @@
     barrier = pltpu.get_barrier_semaphore()
     for partner in partners:
         pl.semaphore_signal(barrier, inc=1, device_id=device(*partner), device_id_type=MESH)
+    loads = [
+        pltpu.make_async_copy(src, dst, load_sem.at[k])
+        for k, (src, dst) in enumerate((
+            (out_ref, out_in), (qkv_ref, qkv_in), (hidden_ref, hidden_in), (gain_ref, gain_in), (bias_hbm, bias_in),
+        ))
+    ]
+    for copy in loads:
+        copy.start()
+
+    def stage(source, first, count):
+        for k in range(count):
+            tiles_ref[first + k] = source[:, k * HD : (k + 1) * HD].reshape(GROUPS, 4, HD)
+
+    def select_rows():
+        wide = hidden_in[...].astype(F32)
+        scale = lax.rsqrt(jnp.sum(wide * wide, axis=1, keepdims=True) * (1.0 / 3584) + norm_eps)
+        base = pl.multiple_of(((7 * seq) // 2) * HD, HD)
+        wide = hidden_in[:, pl.ds(base, 512)].astype(F32) * scale * gain_in[:, pl.ds(base, 512)].astype(F32)
+        near[0:4] = wide
+        near[4:8] = jnp.zeros((4, 512), F32)
+        lhs = near[...].astype(BF16)
+        feature = lax.broadcasted_iota(jnp.int32, (512, 8 * ROWS), 0) + (base - seq * 448)
+        column = lax.broadcasted_iota(jnp.int32, (512, 8 * ROWS), 1)
+        wanted = column + (column // ROWS) * ROWS
+        for k, r in ((0, roll), (1, 1 - roll)):
+            picked = jnp.where(feature == wanted + r * ROWS, 1.0, 0.0).astype(BF16)
+            normed_ref[k] = jnp.dot(lhs, picked, preferred_element_type=F32).astype(BF16)
+
+    def tables():
+        lane = lax.broadcasted_iota(jnp.int32, (4, HD), 1)
+        row = lax.broadcasted_iota(jnp.int32, (4, HD), 0)
+        freq = jnp.zeros((4, HD), F32)
+        for k, value in enumerate(frequencies(HD)):
+            freq = jnp.where(lane % 64 == k, jnp.float32(value), freq)
+        for k in range(3):
+            position = jnp.zeros((4, HD), jnp.int32)
+            for r in range(4):
+                here = len_ref[r] % STRETCH if k == 0 else pos_ref[r, k - 1]
+                position = jnp.where(row == r, here, position)
+            angle = position.astype(F32) * freq
+            turn_ref[k, 0] = jnp.cos(angle)
+            sine = jnp.sin(angle)
+            turn_ref[k, 1] = jnp.where(lane < 64, -sine, sine)
 
     def tiles_of(kind, ty, tcore):
         t = ty * 2 + tcore
@@ -103,32 +139,47 @@
         to, _ = place_of(kind, tcore)
         src = tiles_ref.at[pl.ds(first, count)]
         dst = w_ref.at[pl.ds(to, count), seq, tp, roll]
-        if (dy, dc) == (0, 0):
-            return pltpu.make_async_copy(src, dst, own_sem.at[kind])
         return remote(src, dst, trade_send.at[kind], trade_recv.at[kind, dy * 2 + dc], (x, ty, z, tcore))
 
     def got_trade(kind):
         to, count = place_of(kind, core)
         for dy, dc in TP_STEPS:
-            if (dy, dc) == (0, 0):
-                traded(kind, 0, 0).wait()
-            else:
+            if (dy, dc) != (0, 0):
                 source = ((y - dy) % 4) * 2 + (core + dc) % 2
                 here = w_ref.at[pl.ds(to, count), seq, source, roll]
                 remote(here, here, trade_send.at[kind], trade_recv.at[kind, dy * 2 + dc], tp_peer(dy, dc)).wait_recv()
 
-    for kind in range(3):
-        traded(kind, 0, 0).start()
+    def keep_own(kind):
+        first, count = tiles_of(kind, y, core)
+        to, _ = place_of(kind, core)
+        for k in range(count):
+            w_ref[to + k, seq, tp, roll] = tiles_ref[first + k]
+
+    loads[0].wait()
+    stage(out_in, 24, 16)
+    keep_own(0)
+    loads[1].wait()
+    stage(qkv_in, 0, 24)
+    keep_own(1)
+    keep_own(2)
+    for k in (2, 3, 4):
+        loads[k].wait()
+    select_rows()
     pl.semaphore_wait(barrier, len(partners))
 
+    for dy, dc in TP_STEPS:
+        if (dy, dc) != (0, 0):
+            traded(0, dy, dc).start()
     across = remote(normed_ref.at[1], other, other_sem.at[0], other_sem.at[1], plane_peer(2, 0))
     across.start()
-    for kind in range(3):
+    for kind in (1, 2):
         for dy, dc in TP_STEPS:
             if (dy, dc) != (0, 0):
                 traded(kind, dy, dc).start()
     for copy in caches:
         copy.start()
+    tables()
+    bias_ref[...] = bias_in[...].astype(F32)
 
     def region(kind, half):
         if kind < 2:
@@ -256,7 +307,7 @@
             total = total + r2[k]
         for k in range(3):
             row = (2 * tp + k) if k < 2 else 16 + 4 * core + y
-            qb[tp, k] = (total[:, k * HD : (k + 1) * HD] + bias_ref[row]).astype(BF16)
+            qb[tp, k] = (total[:, k * HD : (k + 1) * HD] + bias_ref[pl.ds(row, 1)]).astype(BF16)
         tp_send(1, lambda t: qb.at[tp], qb.at[tp], recv3)
 
     def turn(v, position):
@@ -416,7 +467,7 @@
     sent_all(5, final_ref, 7)
 
 
-def layer(tiles, normed, bias, turns, lengths, keys, values):
+def layer(hidden, gain, bias, qkv_rows, out_rows, lengths, positions, keys, values):
     hbm, vmem = pl.BlockSpec(memory_space=pltpu.HBM), pl.BlockSpec(memory_space=pltpu.VMEM)
     smem, dma = pl.BlockSpec(memory_space=pltpu.SMEM), pltpu.SemaphoreType.DMA
     return pl.pallas_call(
@@ -427,11 +478,21 @@
             jax.ShapeDtypeStruct((4, 2 * KVH * HD), BF16),
             jax.ShapeDtypeStruct((8, 4, 512), BF16),
         ),
-        in_specs=[hbm, vmem, vmem, vmem, smem, hbm, hbm],
+        in_specs=[hbm, hbm, hbm, hbm, hbm, smem, smem, hbm, hbm],
         out_specs=(vmem, vmem, vmem),
         scratch_shapes=[
+            pltpu.VMEM((4, 3584), BF16),
+            pltpu.VMEM((1, 3584), BF16),
+            pltpu.VMEM((24, HD), BF16),
+            pltpu.VMEM((ROWS, 24 * HD), BF16),
+            pltpu.VMEM((ROWS, 16 * HD), BF16),
+            pltpu.VMEM((40, GROUPS, 4, HD), BF16),
+            pltpu.VMEM((8, 512), F32),
+            pltpu.VMEM((24, HD), F32),
+            pltpu.VMEM((3, 2, 4, HD), F32),
             pltpu.VMEM((4, HERE, KVH * HD), BF16),
             pltpu.VMEM((4, HERE, KVH * HD), BF16),
+            pltpu.VMEM((2, 8, 8 * ROWS), BF16),
             pltpu.VMEM((8, 8 * ROWS), BF16),
             pltpu.VMEM((8 * ROWS, 3 * HD), BF16),
             pltpu.VMEM((2, 4, 3 * HD), F32),
@@ -447,11 +508,45 @@
             pltpu.VMEM((8, 3, 8, HD), F32),
             pltpu.VMEM((8, 4, 512), F32),
             pltpu.VMEM((8, 4, 512), F32),
-            dma((2, 4)), dma((3,)), dma((3,)), dma((3, 8)), dma((3,)), dma((3, 40)), dma((2,)), dma((2,)),
+            dma((5,)), dma((2, 4)), dma((3,)), dma((3, 8)), dma((3,)), dma((3, 40)), dma((2,)), dma((2,)),
             dma((6,)), dma((16,)), dma((8,)), dma((8,)), dma((8,)), dma((8,)), dma((8,)),
         ],
-        compiler_params=pltpu.CompilerParams(collective_id=0, has_side_effects=True, vmem_limit_bytes=36 * 2**20),
-    )(tiles, normed, bias, turns, lengths, keys, values)
+        compiler_params=pltpu.CompilerParams(
+            collective_id=0, has_side_effects=True, vmem_limit_bytes=40 * 2**20
+        ),
+    )(hidden, gain, bias, qkv_rows, out_rows, lengths, positions, keys, values)
+
+
+def place_kernel(w_ref, fresh_ref, final_ref, attended_ref, fresh_out, qkv_ref, out_ref, sems):
+    copies = []
+    for k in range(6):
+        target = out_ref.at[:, k * HD : (k + 1) * HD] if k < 2 else qkv_ref.at[:, (k - 2) * HD : (k - 1) * HD]
+        copies.append(pltpu.make_async_copy(w_ref.at[k], target, sems.at[k]))
+    for copy in copies:
+        copy.start()
+    fresh_out[...] = fresh_ref[...]
+    for o in range(8):
+        attended_ref[:, o * 448 : (o + 1) * 448] = final_ref[o, :, 0:448]
+    for copy in copies:
+        copy.wait()
+
+
+def place(w, fresh, final):
+    hbm, vmem = pl.BlockSpec(memory_space=pltpu.HBM), pl.BlockSpec(memory_space=pltpu.VMEM)
+    return pl.pallas_call(
+        place_kernel,
+        name="place",
+        out_shape=(
+            jax.ShapeDtypeStruct((4, 3584), BF16),
+            jax.ShapeDtypeStruct((4, 1024), BF16),
+            jax.ShapeDtypeStruct((3584, 512), BF16),
+            jax.ShapeDtypeStruct((3584, 256), BF16),
+        ),
+        in_specs=[vmem, vmem, vmem],
+        out_specs=(vmem, vmem, hbm, hbm),
+        scratch_shapes=[pltpu.SemaphoreType.DMA((6,))],
+        compiler_params=pltpu.CompilerParams(vmem_limit_bytes=8 * 2**20),
+    )(w, fresh, final)
 
 
 def body(
@@ -465,30 +560,11 @@
     cache_len,
     block_pos,
 ):
-    rollouts = hidden.shape[0]
-    rows = jnp.concatenate([qkv_weight, out_weight], axis=1).reshape(ROWS, 40, HD)
-    tiles = jnp.transpose(rows, (1, 0, 2)).reshape(40, GROUPS, 4, HD)
-    normed = normalize(hidden, norm_gain)
-    near = lax.dynamic_slice_in_dim(normed, lax.axis_index(SEQ) * 448, 448, 1)
-    near = near.reshape(rollouts, 8, 2, ROWS)
-    odd = lax.axis_index("roll") == 1
-    even_rows, odd_rows = (near[:, :, k].reshape(rollouts, 8 * ROWS) for k in (0, 1))
-    chosen = jnp.stack([jnp.where(odd, odd_rows, even_rows), jnp.where(odd, even_rows, odd_rows)])
-    chosen = jnp.pad(chosen, ((0, 0), (0, 4), (0, 0)))
-    bias = qkv_bias.astype(F32).reshape(24, 1, HD)
-    inverse = jnp.asarray(frequencies(HD), dtype=F32)
-    positions = jnp.concatenate([(cache_len % STRETCH)[:, None], block_pos], axis=1)
-    angles = positions.T.astype(F32)[..., None] * inverse
-    cosine, sine = jnp.cos(angles), jnp.sin(angles)
-    turns = jnp.stack(
-        [jnp.concatenate([cosine, cosine], axis=-1), jnp.concatenate([-sine, sine], axis=-1)], axis=1
-    )
-    w, fresh_kv, final = layer(tiles, chosen, bias, turns, cache_len, key_cache, value_cache)
-    joint = w.reshape(6, 3584, HD)
-    served_out = jnp.moveaxis(joint[:2], 0, 1).reshape(3584, 2 * HD)
-    served_qkv = jnp.moveaxis(joint[2:], 0, 1).reshape(3584, 4 * HD)
-    attended = jnp.moveaxis(final[:, :, :448], 0, 1).reshape(rollouts, 3584)
-    return (attended, fresh_kv, served_qkv, served_out)
+    fixed = (hidden, norm_gain.reshape(1, 3584), qkv_bias.reshape(24, HD), qkv_weight, out_weight)
+    fixed = [pltpu.with_memory_space_constraint(a, pltpu.HBM) for a in fixed]
+    caches = [pltpu.with_memory_space_constraint(a, pltpu.HBM) for a in (key_cache, value_cache)]
+    w, fresh_kv, final = layer(*fixed, cache_len, block_pos, *caches)
+    return place(w.reshape(6, 3584, HD), fresh_kv, final)
 
 
 def solution(mesh):

time: 76.1 us -> 55.8 us (0.73)
  local copies, waits for them, and re-layouts: 19.9 us -> 2.73 us
  other arithmetic: 5.8 us -> 0 us
  Pallas kernels: 49.1 us -> 52.3 us
    unnamed x10 -> x3, local copies, waits for them, and re-layouts: 8.05 us -> 1.42 us
    slice x2 -> x0, local copies, waits for them, and re-layouts: 5.93 us -> none  [the longest x1 3.76 us: body(): served_qkv = jnp.moveaxis(joint[2:], 0, 1).reshape(3584, 4 * HD)]
    reshape x6 -> x1, local copies, waits for them, and re-layouts: 4.97 us -> 1.3 us  [body(): norm_gain.reshape(1, 3584)]
    pallas_call x0 -> x1, Pallas kernels: none -> 3.1 us  [place(): pl.pallas_call(place_kernel, name='place', out_shape=(jax.ShapeDtypeStruc...]
    convert_element_type x3 -> x0, other arithmetic: 1.52 us -> none  [the longest x1 0.76 us: normalize(): wide_rows = row_block.astype(F32)]
    concatenate x1 -> x0, other arithmetic: 1.02 us -> none  [body(): jnp.concatenate([qkv_weight, out_weight], axis=1).reshape(ROWS, 40, HD)]
    reduce_sum x1 -> x0, other arithmetic: 0.89 us -> none  [normalize(): jnp.mean(wide_rows * wide_rows, axis=1, keepdims=True) + norm_eps]
    cos x1 -> x0, other arithmetic: 0.78 us -> none  [body(): cosine, sine = (jnp.cos(angles), jnp.sin(angles))]
where the time goes in v3:
time: 55.8 us; the launch traced here: 55.6 us
  Pallas kernels  52.3 us (94%)
  local copies, waits for them, and re-layouts  2.73 us (5%)
  between operations  0.64 us (1%)
    pallas_call x1, Pallas kernels, layer(): pl.pallas_call(layer_kernel, name='layer', out_shape=(jax.ShapeDtypeStruc...  49.2 us
    pallas_call x1, Pallas kernels, place(): pl.pallas_call(place_kernel, name='place', out_shape=(jax.ShapeDtypeStruc...  3.1 us
    unnamed x3, local copies, waits for them, and re-layouts  1.42 us
    reshape x1, local copies, waits for them, and re-layouts, body(): norm_gain.reshape(1, 3584)  1.3 us

profile of v3, /device:TPU:1, one launch (start us, length us, event | category | flops | bytes accessed | tf_op | source)
XLA Modules:
  0.0 55.6 jit_solution(10475297836327203408)
XLA Ops:
  0.6 0.8 %copy.13.pos_ref = s32[4,2]{1,0:T(4,128)S(1)} copy(s32[4,2]{0,1:T(2,128)} %param.17) | data formatting | bytes 64 | tf_op args[8]
  1.4 1.3 %reshape.17.gain_ref = bf16[1,3584]{1,0:T(2,128)(2,1)} reshape(bf16[3584]{0:T(1024)(128)(2,1)} %param.10) | data formatting | bytes 14336 | tf_op jit(solution)/shard_map/reshape | solution.py:563
  2.7 0.0 copy-start
  2.7 0.7 %copy-done = s32[4]{0:T(128)S(1)} copy-done((s32[4]{0:T(128)S(1)}, s32[4]{0:T(128)}, u32[]{:S(2)}) %copy-start) | copy-done | bytes 40
  3.4 49.2 %layer.1 = (bf16[6,8,8,2,7,4,128]{6,5,4,3,2,1,0:T(4,128)(2,1)S(1)}, bf16[4,1024]{1,0:T(4,128)(2,1)S(1)}, bf16[8,4,512]{2,1,0:T(4,128)(2,1)S(1)}) custom-call(bf16[4,3584]{1,0:T(4,128)(2,1)} %hidden_ref.1, bf16[1,3584]{1,0:T(2,128)(2,1)} %reshape.17.gain_ref, bf16[24,128]{1,0:T(8,128)(2,1)} %bitcast.3, bf16[28,3072]{1,0:T(8,128)(2,1)} %qkv_ref.1, ...), custom_call_target="tpu_custom_call" | custom-call | tf_op jit(solution)/shard_map/layer/pallas_call | solution.py:473
  52.5 3.1 %place.1 = (bf16[4,3584]{1,0:T(4,128)(2,1)}, bf16[4,1024]{1,0:T(4,128)(2,1)}, bf16[3584,512]{1,0:T(8,128)(2,1)}, bf16[3584,256]{1,0:T(8,128)(2,1)}) custom-call(bf16[6,3584,128]{2,1,0:T(8,128)(2,1)S(1)} %bitcast.2, bf16[4,1024]{1,0:T(4,128)(2,1)S(1)} %get-tuple-element.8.fresh_ref, bf16[8,4,512]{2,1,0:T(4,128)(2,1)S(1)} %get-tuple-element.9.final_ref), custom_call_target="tpu_custom_call" | custom-call | tf_op jit(solution)/shard_map/place/pallas_call | solution.py:536
Async XLA Ops:
  2.7 0.7 %copy-start = (s32[4]{0:T(128)S(1)}, s32[4]{0:T(128)}, u32[]{:S(2)}) copy-start(s32[4]{0:T(128)} %len_ref.1) | copy-start | bytes 52

commit v4 on v3

--- a/solution.py
+++ b/solution.py
@@ -13,6 +13,7 @@
 BLOCK = 512
 STRETCH = 8192
 ROWS = 28
+PLACE = 4
 GROUPS = 7
 HERE = 1024
 TP = ("tp_0", "tp_1")
@@ -46,12 +47,29 @@
 PLANE_STEPS = tuple((dx, dz) for dx in (2, 1, 3, 0) for dz in (2, 1, 3, 0))
 
 
+STEPS = (
+    ("ownA", 1), ("ownA", 0), ("ownB", 1), ("ownB", 2), ("ownB", 0), ("project",), ("f1m", 2, 1),
+    ("f1m", 2, 0), ("f1p", 2, 1), ("f1m", 0, 0), ("f1m", 0, 1), ("f1p", 0, 0), ("share",), ("f1p", 0, 1),
+    ("f2", 2, 1), ("f1p", 1, 1), ("gm", 0, 1, 0), ("f1m", 1, 0), ("gm", 0, 0, 0), ("f1p", 2, 0),
+    ("gp", 0, 0, 1), ("f2", 0, 0), ("gp", 0, 0, 0), ("gp", 0, 1, 0), ("queries",), ("f1p", 1, 0),
+    ("f2", 0, 1), ("scores",), ("gm", 0, 1, 1), ("gm", 0, 0, -1), ("gp", 0, 1, 1), ("values",),
+    ("gp", 0, 1, -1), ("gp", 0, 0, -1), ("f1m", 1, 1), ("gm", 0, 1, -1), ("gp", 2, 1, -1), ("f2", 2, 0),
+    ("gm", 0, 0, 2), ("gp", 0, 0, 2), ("gm", 0, 0, 1), ("gp", 0, 1, 2), ("gm", 0, 1, 2), ("gm", 2, 1, 0),
+    ("gm", 2, 0, 1), ("over_tp",), ("f2", 1, 0), ("gp", 2, 0, 1), ("f2", 1, 1), ("gm", 2, 1, 1),
+    ("gp", 1, 0, 1), ("gp", 2, 1, 1), ("gm", 1, 1, -1), ("gm", 1, 0, 1), ("gp", 1, 1, 0), ("gm", 1, 0, 0),
+    ("gm", 2, 0, 0), ("gp", 2, 0, 2), ("gp", 1, 1, 1), ("gm", 2, 1, -1), ("gp", 2, 1, 2), ("gm", 1, 1, 1),
+    ("gp", 1, 0, 0), ("gp", 2, 0, 0), ("gm", 1, 1, 0), ("gm", 1, 0, -1), ("gm", 2, 0, 2), ("gp", 1, 0, -1),
+    ("stage_out",), ("out_project",), ("gm", 2, 1, 2), ("gp", 2, 1, 0), ("gp", 1, 1, -1), ("gm", 2, 0, -1),
+    ("gp", 2, 0, -1), ("gp", 1, 0, 2), ("gp", 1, 1, 2), ("gm", 1, 1, 2), ("gm", 1, 0, 2), ("reduce_out",),
+)
+
+
 def layer_kernel(
     hidden_ref, gain_ref, bias_hbm, qkv_ref, out_ref, len_ref, pos_ref, key_ref, value_ref,
     w_ref, fresh_ref, final_ref,
-    hidden_in, gain_in, bias_in, qkv_in, out_in, tiles_ref, near, bias_ref, turn_ref,
-    kbuf, vbuf, normed_ref, other, wq, part, r2, qb, rot, self_s, s_buf, p_buf, ob, r5, c6, r6, po, r7,
-    load_sem, cache_sem, trade_send, trade_recv, ring_send, ring_recv, pair_sem, other_sem,
+    len_smem, pos_smem, hidden_in, gain_in, gain_row, bias_in, qkv_in, out_in, tiles_ref, near, bias_ref, turn_ref,
+    kbuf, vbuf, normed_ref, other, wo, wq, part, r2, qb, rot, self_s, s_buf, p_buf, ob, r5, c6, r6, po, r7,
+    line_sem, load_sem, cache_sem, trade_send, trade_recv, ring_send, ring_recv, pair_sem, other_sem,
     stage_send, recv2, recv3, recv5, recv6, recv7, recv8,
 ):
     x = lax.axis_index("roll") * 2 + lax.axis_index("seq_0")
@@ -71,7 +89,7 @@
         return ((x + dx) % 4, y, (z + dz) % 4, core)
 
     partners = [tp_peer(dy, dc) for dy, dc in TP_STEPS if (dy, dc) != (0, 0)]
-    partners += [plane_peer(dx, dz) for dx, dz in PLANE_STEPS if (dx, dz) != (0, 0)]
+    partners += [plane_peer(dx, dz) for dx, dz in PLANE_STEPS if (dx == 0) != (dz == 0)]
 
     caches = []
     for r in range(4):
@@ -86,6 +104,7 @@
         pltpu.make_async_copy(src, dst, load_sem.at[k])
         for k, (src, dst) in enumerate((
             (out_ref, out_in), (qkv_ref, qkv_in), (hidden_ref, hidden_in), (gain_ref, gain_in), (bias_hbm, bias_in),
+            (len_ref, len_smem), (pos_ref, pos_smem),
         ))
     ]
     for copy in loads:
@@ -98,8 +117,9 @@
     def select_rows():
         wide = hidden_in[...].astype(F32)
         scale = lax.rsqrt(jnp.sum(wide * wide, axis=1, keepdims=True) * (1.0 / 3584) + norm_eps)
+        gain_row[...] = gain_in[...].astype(F32).reshape(1, 3584)
         base = pl.multiple_of(((7 * seq) // 2) * HD, HD)
-        wide = hidden_in[:, pl.ds(base, 512)].astype(F32) * scale * gain_in[:, pl.ds(base, 512)].astype(F32)
+        wide = hidden_in[:, pl.ds(base, 512)].astype(F32) * scale * gain_row[:, pl.ds(base, 512)]
         near[0:4] = wide
         near[4:8] = jnp.zeros((4, 512), F32)
         lhs = near[...].astype(BF16)
@@ -119,7 +139,7 @@
         for k in range(3):
             position = jnp.zeros((4, HD), jnp.int32)
             for r in range(4):
-                here = len_ref[r] % STRETCH if k == 0 else pos_ref[r, k - 1]
+                here = len_smem[r] % STRETCH if k == 0 else pos_smem[k - 1, r]
                 position = jnp.where(row == r, here, position)
             angle = position.astype(F32) * freq
             turn_ref[k, 0] = jnp.cos(angle)
@@ -141,9 +161,9 @@
         dst = w_ref.at[pl.ds(to, count), seq, tp, roll]
         return remote(src, dst, trade_send.at[kind], trade_recv.at[kind, dy * 2 + dc], (x, ty, z, tcore))
 
-    def got_trade(kind):
+    def got_trade(kind, steps):
         to, count = place_of(kind, core)
-        for dy, dc in TP_STEPS:
+        for dy, dc in steps:
             if (dy, dc) != (0, 0):
                 source = ((y - dy) % 4) * 2 + (core + dc) % 2
                 here = w_ref.at[pl.ds(to, count), seq, source, roll]
@@ -162,19 +182,20 @@
     stage(qkv_in, 0, 24)
     keep_own(1)
     keep_own(2)
-    for k in (2, 3, 4):
+    for k in range(2, 7):
         loads[k].wait()
     select_rows()
     pl.semaphore_wait(barrier, len(partners))
-
-    for dy, dc in TP_STEPS:
-        if (dy, dc) != (0, 0):
-            traded(0, dy, dc).start()
+    for dx in (1, 2, 3):
+        pl.semaphore_signal(line_sem, inc=1, device_id=device(*plane_peer(dx, 0)), device_id_type=MESH)
+
+    for kind in (1, 2, 0):
+        traded(kind, 0, 1).start()
     across = remote(normed_ref.at[1], other, other_sem.at[0], other_sem.at[1], plane_peer(2, 0))
     across.start()
-    for kind in (1, 2):
+    for kind in (1, 2, 0):
         for dy, dc in TP_STEPS:
-            if (dy, dc) != (0, 0):
+            if dy != 0:
                 traded(kind, dy, dc).start()
     for copy in caches:
         copy.start()
@@ -213,44 +234,54 @@
         ring(kind, half, k, f, 0, None, (0, 1)).start()
         ring(kind, half, k + 1, f, 0, None, (0, -1)).start()
 
-    def s1(kind):
-        for half in (0, 1):
-            ring(kind, half, 0, 0, 0, None, (1, 0)).start()
-            ring(kind, half, 1, 0, 0, None, (-1, 0)).start()
-        for half in (0, 1):
-            sideways(kind, half, 0)
-            to_pair(kind, half, 0, 0)
-
-    def s2(kind):
-        for half in (0, 1):
-            ring(kind, half, 0, -1, 0, None, (1, 0)).wait_recv()
-            ring(kind, half, 2, -1, 0, 0, (1, 0)).start()
-            ring(kind, half, 1, 1, 0, None, (1, 0)).wait_recv()
-            ring(kind, half, 3, 1, 0, 1, (-1, 0)).start()
-        for half in (0, 1):
-            for f in (-1, 1):
-                sideways(kind, half, f)
-                to_pair(kind, half, f, 0)
-
-    def s3(kind):
-        for half in (0, 1):
-            ring(kind, half, 2, 2, 0, 0, (1, 0)).wait_recv()
-            ring(kind, half, 3, 2, 0, 1, (1, 0)).wait_recv()
-            sideways(kind, half, 2)
-            to_pair(kind, half, 2, 0)
-
-    def s4(kind, fs=ORDER):
-        for f in fs:
+    def own_rows(kind, dys):
+        for message, along in ((0, (1, 0)), (1, (-1, 0)), (4, (0, 1)), (5, (0, -1))):
             for half in (0, 1):
-                k = 4 + ORDER.index(f) * 4
-                ring(kind, half, k, f, -1, None, (0, 1)).wait_recv()
-                ring(kind, half, k + 2, f, -1, 0, (0, 1)).start()
-                to_pair(kind, half, f, -1)
-                ring(kind, half, k + 1, f, 1, None, (0, 1)).wait_recv()
-                ring(kind, half, k + 3, f, 1, 1, (0, -1)).start()
-                to_pair(kind, half, f, 1)
-
-    def s5(kind):
+                tx, tz = coords(half, *along)
+                tile, _, _ = region(kind, half)
+                for dy in dys:
+                    first = ((y - dy) % 4) * 2
+                    block = w_ref.at[pl.ds(tile, 1), seq, pl.ds(first, 2), roll]
+                    if kind == 2:
+                        continue
+                    remote(
+                        block, block, ring_send.at[kind], ring_recv.at[kind, half * 20 + message], (tx, y, tz, core)
+                    ).start()
+                if kind == 2 and 0 not in dys:
+                    block = block_at(kind, half, x, z, None)
+                    remote(
+                        block, block, ring_send.at[kind], ring_recv.at[kind, half * 20 + message], (tx, y, tz, core)
+                    ).start()
+        if kind == 2 and 0 not in dys:
+            for half in (0, 1):
+                to_pair(kind, half, 0, 0)
+
+    def first_step(kind, half, f):
+        ring(kind, half, 0 if f < 0 else 1, f, 0, None, (1, 0)).wait_recv()
+        if f < 0:
+            ring(kind, half, 2, f, 0, 0, (1, 0)).start()
+        else:
+            ring(kind, half, 3, f, 0, 1, (-1, 0)).start()
+        sideways(kind, half, f)
+        to_pair(kind, half, f, 0)
+
+    def far_step(kind, half):
+        ring(kind, half, 2, 2, 0, 0, (1, 0)).wait_recv()
+        ring(kind, half, 3, 2, 0, 1, (1, 0)).wait_recv()
+        sideways(kind, half, 2)
+        to_pair(kind, half, 2, 0)
+
+    def side_step(kind, half, f, g):
+        k = 4 + ORDER.index(f) * 4
+        if g < 0:
+            ring(kind, half, k, f, -1, None, (0, 1)).wait_recv()
+            ring(kind, half, k + 2, f, -1, 0, (0, 1)).start()
+        else:
+            ring(kind, half, k + 1, f, 1, None, (0, 1)).wait_recv()
+            ring(kind, half, k + 3, f, 1, 1, (0, -1)).start()
+        to_pair(kind, half, f, g)
+
+    def last_step(kind):
         for f in ORDER:
             for half in (0, 1):
                 k = 4 + ORDER.index(f) * 4
@@ -258,6 +289,8 @@
                 to_pair(kind, half, f, 2, 0)
                 ring(kind, half, k + 3, f, 2, 1, (0, 1)).wait_recv()
                 to_pair(kind, half, f, 2, 1)
+
+    def sent_ring(kind):
         sent = w_ref.at[0:5, 0 : (6 if kind < 2 else 3), :, 0]
         remote(sent, sent, ring_send.at[kind], ring_recv.at[kind, 0], plane_peer(0, 1)).wait_send()
 
@@ -278,8 +311,6 @@
         remote(sent, sent, stage_send.at[stage], recv3.at[0], tp_peer(0, 1)).wait_send()
 
     def project():
-        got_trade(1)
-        got_trade(2)
         across.wait_recv()
         for k in range(3):
             tile = (2 + k) if k < 2 else 4 + core
@@ -289,6 +320,7 @@
             made = jnp.dot(lhs, wq[...], preferred_element_type=F32)
             part[k] = made[0:4]
         r2[x * 4 + z] = part[0]
+        pl.semaphore_wait(line_sem, 3)
         for dx, dz in PLANE_STEPS:
             if (dx, dz) != (0, 0):
                 tx, _, tz, _ = plane_peer(dx, dz)
@@ -334,7 +366,7 @@
         for r in range(4):
             caches[r].wait()
             for b in range(2):
-                valid = (owner == r) & (column + (start + b * BLOCK) < len_ref[r])
+                valid = (owner == r) & (column + (start + b * BLOCK) < len_smem[r])
                 for g in range(KVH):
                     rows, cols = slice(16 * g, 16 * g + 16), slice(b * BLOCK, (b + 1) * BLOCK)
                     made = lax.dot_general(
@@ -407,12 +439,16 @@
         attention = (numerator / (old_low * factor + fresh)).astype(BF16)
         return attention
 
+    def stage_out():
+        for o in range(8):
+            for k in range(2):
+                wo[k, o] = w_ref[k, o].reshape(16 * ROWS, HD)
+
     def out_project(attention):
         for o in range(8):
             sums = []
             for k in range(2):
-                rows = w_ref[k, o].reshape(16 * ROWS, HD)
-                sums.append(lax.dot_general(attention, rows, (((1,), (1,)), ((), ())), preferred_element_type=F32))
+                sums.append(lax.dot_general(attention, wo[k, o], (((1,), (1,)), ((), ())), preferred_element_type=F32))
             po[o, :, 0:448] = sums[0][0:4] + sums[1][4:8]
             po[o, :, 448:512] = jnp.zeros((4, 64), F32)
         r7[tp] = po[tp]
@@ -426,30 +462,57 @@
         final_ref[tp] = total.astype(BF16)
         tp_send(5, lambda t: final_ref.at[tp], final_ref.at[tp], recv8)
 
-    got_trade(0)
-    s1(0)
-    project()
-    s1(1)
-    s2(0)
-    share()
-    s3(0)
-    s1(2)
-    queries()
-    s2(1)
-    scores()
-    s4(0)
-    values()
-    s3(1)
-    s2(2)
-    over_tp()
-    s5(0)
-    s4(1)
-    out_project(finish())
-    s3(2)
-    s4(2)
-    reduce_out()
-    s5(1)
-    s5(2)
+    pair, rest = ((0, 1),), tuple((dy, dc) for dy, dc in TP_STEPS if dy)
+    had = set()
+
+    def need(kind, *parts):
+        for name, steps in (("pair", pair), ("rest", rest)):
+            if name in parts and (kind, name) not in had:
+                had.add((kind, name))
+                got_trade(kind, steps)
+
+    for name, *at in STEPS:
+        if name == "ownA":
+            need(at[0], "pair")
+            own_rows(at[0], (0,))
+        elif name == "ownB":
+            need(at[0], "pair", "rest")
+            own_rows(at[0], (3, 1, 2))
+        elif name == "f1p":
+            first_step(*at, -1)
+        elif name == "f1m":
+            first_step(*at, 1)
+        elif name == "f2":
+            far_step(*at)
+        elif name == "gp":
+            side_step(*at, -1)
+        elif name == "gm":
+            side_step(*at, 1)
+        elif name == "project":
+            need(1, "pair", "rest")
+            need(2, "pair", "rest")
+            project()
+        elif name == "share":
+            share()
+        elif name == "queries":
+            queries()
+        elif name == "scores":
+            scores()
+        elif name == "values":
+            values()
+        elif name == "over_tp":
+            over_tp()
+        elif name == "stage_out":
+            last_step(0)
+            stage_out()
+        elif name == "out_project":
+            out_project(finish())
+        elif name == "reduce_out":
+            reduce_out()
+    last_step(1)
+    last_step(2)
+    for kind in range(3):
+        sent_ring(kind)
     tile = w_ref.at[5 - core]
     whole = remote(tile, tile, pair_sem.at[0], pair_sem.at[1], tp_peer(0, 1))
     whole.wait_send()
@@ -469,7 +532,7 @@
 
 def layer(hidden, gain, bias, qkv_rows, out_rows, lengths, positions, keys, values):
     hbm, vmem = pl.BlockSpec(memory_space=pltpu.HBM), pl.BlockSpec(memory_space=pltpu.VMEM)
-    smem, dma = pl.BlockSpec(memory_space=pltpu.SMEM), pltpu.SemaphoreType.DMA
+    dma = pltpu.SemaphoreType.DMA
     return pl.pallas_call(
         layer_kernel,
         name="layer",
@@ -478,11 +541,14 @@
             jax.ShapeDtypeStruct((4, 2 * KVH * HD), BF16),
             jax.ShapeDtypeStruct((8, 4, 512), BF16),
         ),
-        in_specs=[hbm, hbm, hbm, hbm, hbm, smem, smem, hbm, hbm],
+        in_specs=[hbm] * 9,
         out_specs=(vmem, vmem, vmem),
         scratch_shapes=[
+            pltpu.SMEM((4,), jnp.int32),
+            pltpu.SMEM((2, 4), jnp.int32),
             pltpu.VMEM((4, 3584), BF16),
-            pltpu.VMEM((1, 3584), BF16),
+            pltpu.VMEM((3584,), BF16),
+            pltpu.VMEM((1, 3584), F32),
             pltpu.VMEM((24, HD), BF16),
             pltpu.VMEM((ROWS, 24 * HD), BF16),
             pltpu.VMEM((ROWS, 16 * HD), BF16),
@@ -494,6 +560,7 @@
             pltpu.VMEM((4, HERE, KVH * HD), BF16),
             pltpu.VMEM((2, 8, 8 * ROWS), BF16),
             pltpu.VMEM((8, 8 * ROWS), BF16),
+            pltpu.VMEM((2, 8, 16 * ROWS, HD), BF16),
             pltpu.VMEM((8 * ROWS, 3 * HD), BF16),
             pltpu.VMEM((2, 4, 3 * HD), F32),
             pltpu.VMEM((16, 4, 3 * HD), F32),
@@ -508,7 +575,7 @@
             pltpu.VMEM((8, 3, 8, HD), F32),
             pltpu.VMEM((8, 4, 512), F32),
             pltpu.VMEM((8, 4, 512), F32),
-            dma((5,)), dma((2, 4)), dma((3,)), dma((3, 8)), dma((3,)), dma((3, 40)), dma((2,)), dma((2,)),
+            pltpu.SemaphoreType.REGULAR, dma((7,)), dma((2, 4)), dma((3,)), dma((3, 8)), dma((3,)), dma((3, 40)), dma((2,)), dma((2,)),
             dma((6,)), dma((16,)), dma((8,)), dma((8,)), dma((8,)), dma((8,)), dma((8,)),
         ],
         compiler_params=pltpu.CompilerParams(
@@ -521,7 +588,9 @@
     copies = []
     for k in range(6):
         target = out_ref.at[:, k * HD : (k + 1) * HD] if k < 2 else qkv_ref.at[:, (k - 2) * HD : (k - 1) * HD]
-        copies.append(pltpu.make_async_copy(w_ref.at[k], target, sems.at[k]))
+        for part in range(PLACE):
+            rows = slice(part * 3584 // PLACE, (part + 1) * 3584 // PLACE)
+            copies.append(pltpu.make_async_copy(w_ref.at[k, rows], target.at[rows], sems.at[k, part]))
     for copy in copies:
         copy.start()
     fresh_out[...] = fresh_ref[...]
@@ -544,7 +613,7 @@
         ),
         in_specs=[vmem, vmem, vmem],
         out_specs=(vmem, vmem, hbm, hbm),
-        scratch_shapes=[pltpu.SemaphoreType.DMA((6,))],
+        scratch_shapes=[pltpu.SemaphoreType.DMA((6, PLACE))],
         compiler_params=pltpu.CompilerParams(vmem_limit_bytes=8 * 2**20),
     )(w, fresh, final)
 
@@ -560,10 +629,11 @@
     cache_len,
     block_pos,
 ):
-    fixed = (hidden, norm_gain.reshape(1, 3584), qkv_bias.reshape(24, HD), qkv_weight, out_weight)
-    fixed = [pltpu.with_memory_space_constraint(a, pltpu.HBM) for a in fixed]
-    caches = [pltpu.with_memory_space_constraint(a, pltpu.HBM) for a in (key_cache, value_cache)]
-    w, fresh_kv, final = layer(*fixed, cache_len, block_pos, *caches)
+    operands = (
+        hidden, norm_gain, qkv_bias.reshape(24, HD), qkv_weight, out_weight,
+        cache_len, block_pos.T, key_cache, value_cache,
+    )
+    w, fresh_kv, final = layer(*(pltpu.with_memory_space_constraint(a, pltpu.HBM) for a in operands))
     return place(w.reshape(6, 3584, HD), fresh_kv, final)
 
 

time: 55.8 us -> 49.8 us (0.89)
  Pallas kernels: 52.3 us -> 49.1 us
  local copies, waits for them, and re-layouts: 2.73 us -> 0 us
    pallas_call x1, Pallas kernels: 49.2 us -> 45.8 us  [layer(): pl.pallas_call(layer_kernel, name='layer', out_shape=(jax.ShapeDtypeStruc...]
    unnamed x3 -> x0, local copies, waits for them, and re-layouts: 1.42 us -> none
    reshape x1 -> x0, local copies, waits for them, and re-layouts: 1.3 us -> none  [body(): norm_gain.reshape(1, 3584)]
where the time goes in v4:
time: 49.8 us; the launch traced here: 49.7 us
  Pallas kernels  49.1 us (99%)
  between operations  0.64 us (1%)
    pallas_call x1, Pallas kernels, layer(): pl.pallas_call(layer_kernel, name='layer', out_shape=(jax.ShapeDtypeStruc...  45.8 us
    pallas_call x1, Pallas kernels, place(): pl.pallas_call(place_kernel, name='place', out_shape=(jax.ShapeDtypeStruc...  3.22 us

profile of v4, /device:TPU:1, one launch (start us, length us, event | category | flops | bytes accessed | tf_op | source)
XLA Modules:
  0.0 49.7 jit_solution(6969161303337052541)
XLA Ops:
  0.6 45.8 %layer.1 = (bf16[6,8,8,2,7,4,128]{6,5,4,3,2,1,0:T(4,128)(2,1)S(1)}, bf16[4,1024]{1,0:T(4,128)(2,1)S(1)}, bf16[8,4,512]{2,1,0:T(4,128)(2,1)S(1)}) custom-call(bf16[4,3584]{1,0:T(4,128)(2,1)} %hidden_ref.1, bf16[3584]{0:T(1024)(128)(2,1)} %gain_ref.1, bf16[24,128]{1,0:T(8,128)(2,1)} %bitcast.4, bf16[28,3072]{1,0:T(8,128)(2,1)} %qkv_ref.1, ...), custom_call_target="tpu_custom_call" | custom-call | tf_op jit(solution)/shard_map/layer/pallas_call | solution.py:536
  46.5 3.2 %place.1 = (bf16[4,3584]{1,0:T(4,128)(2,1)}, bf16[4,1024]{1,0:T(4,128)(2,1)}, bf16[3584,512]{1,0:T(8,128)(2,1)}, bf16[3584,256]{1,0:T(8,128)(2,1)}) custom-call(bf16[6,3584,128]{2,1,0:T(8,128)(2,1)S(1)} %bitcast.3, bf16[4,1024]{1,0:T(4,128)(2,1)S(1)} %get-tuple-element.8.fresh_ref, bf16[8,4,512]{2,1,0:T(4,128)(2,1)S(1)} %get-tuple-element.9.final_ref), custom_call_target="tpu_custom_call" | custom-call | tf_op jit(solution)/shard_map/place/pallas_call | solution.py:605

commit v5 on v4

--- a/solution.py
+++ b/solution.py
@@ -48,19 +48,19 @@
 
 
 STEPS = (
-    ("ownA", 1), ("ownA", 0), ("ownB", 1), ("ownB", 2), ("ownB", 0), ("project",), ("f1m", 2, 1),
-    ("f1m", 2, 0), ("f1p", 2, 1), ("f1m", 0, 0), ("f1m", 0, 1), ("f1p", 0, 0), ("share",), ("f1p", 0, 1),
-    ("f2", 2, 1), ("f1p", 1, 1), ("gm", 0, 1, 0), ("f1m", 1, 0), ("gm", 0, 0, 0), ("f1p", 2, 0),
-    ("gp", 0, 0, 1), ("f2", 0, 0), ("gp", 0, 0, 0), ("gp", 0, 1, 0), ("queries",), ("f1p", 1, 0),
-    ("f2", 0, 1), ("scores",), ("gm", 0, 1, 1), ("gm", 0, 0, -1), ("gp", 0, 1, 1), ("values",),
-    ("gp", 0, 1, -1), ("gp", 0, 0, -1), ("f1m", 1, 1), ("gm", 0, 1, -1), ("gp", 2, 1, -1), ("f2", 2, 0),
-    ("gm", 0, 0, 2), ("gp", 0, 0, 2), ("gm", 0, 0, 1), ("gp", 0, 1, 2), ("gm", 0, 1, 2), ("gm", 2, 1, 0),
-    ("gm", 2, 0, 1), ("over_tp",), ("f2", 1, 0), ("gp", 2, 0, 1), ("f2", 1, 1), ("gm", 2, 1, 1),
-    ("gp", 1, 0, 1), ("gp", 2, 1, 1), ("gm", 1, 1, -1), ("gm", 1, 0, 1), ("gp", 1, 1, 0), ("gm", 1, 0, 0),
-    ("gm", 2, 0, 0), ("gp", 2, 0, 2), ("gp", 1, 1, 1), ("gm", 2, 1, -1), ("gp", 2, 1, 2), ("gm", 1, 1, 1),
-    ("gp", 1, 0, 0), ("gp", 2, 0, 0), ("gm", 1, 1, 0), ("gm", 1, 0, -1), ("gm", 2, 0, 2), ("gp", 1, 0, -1),
-    ("stage_out",), ("out_project",), ("gm", 2, 1, 2), ("gp", 2, 1, 0), ("gp", 1, 1, -1), ("gm", 2, 0, -1),
-    ("gp", 2, 0, -1), ("gp", 1, 0, 2), ("gp", 1, 1, 2), ("gm", 1, 1, 2), ("gm", 1, 0, 2), ("reduce_out",),
+    ("ownA", 1), ("ownA", 0), ("ownB", 1), ("ownB", 2), ("ownB", 0), ("project",), ("gp", 2, 0, 0),
+    ("f1m", 0, 1), ("f1p", 0, 0), ("f1p", 0, 1), ("gm", 1, 0, 0), ("gp", 0, 1, 0), ("gp", 2, 1, 0),
+    ("f1m", 0, 0), ("f1m", 2, 0), ("f1p", 1, 1), ("share",), ("f1m", 1, 1), ("f1p", 2, 0), ("f2", 0, 1),
+    ("f1m", 1, 0), ("f1p", 2, 1), ("gp", 0, 1, -1), ("f1m", 2, 1), ("gm", 0, 1, 0), ("f2", 0, 0),
+    ("gm", 0, 0, 1), ("f1p", 1, 0), ("gm", 0, 1, -1), ("gp", 0, 1, 1), ("gp", 0, 0, -1), ("gm", 2, 0, 0),
+    ("queries",), ("scores",), ("values",), ("gm", 0, 0, 0), ("gm", 0, 0, -1), ("f2", 1, 1), ("gp", 2, 0, -1),
+    ("f2", 2, 0), ("gp", 0, 0, 2), ("gm", 0, 1, 2), ("gp", 0, 0, 0), ("gp", 0, 1, 2), ("f2", 2, 1),
+    ("gm", 0, 0, 2), ("gp", 0, 0, 1), ("gm", 0, 1, 1), ("over_tp",), ("f2", 1, 0), ("gp", 2, 1, 1),
+    ("gm", 2, 0, -1), ("gm", 1, 1, 1), ("gm", 1, 1, 2), ("gp", 2, 1, -1), ("gp", 2, 0, 2), ("gp", 1, 0, 0),
+    ("gp", 1, 1, 1), ("gm", 1, 1, -1), ("gm", 2, 1, 0), ("gp", 1, 0, 1), ("gm", 2, 1, 1), ("gm", 2, 0, 2),
+    ("gp", 1, 1, 0), ("gm", 1, 0, -1), ("gm", 2, 1, -1), ("gp", 1, 0, -1), ("gp", 1, 1, -1), ("stage_out",),
+    ("out_project",), ("gm", 2, 0, 1), ("gp", 2, 0, 1), ("gm", 1, 1, 0), ("gp", 2, 1, 2), ("gm", 1, 0, 1),
+    ("gp", 1, 1, 2), ("gm", 2, 1, 2), ("gp", 1, 0, 2), ("gm", 1, 0, 2), ("reduce_out",),
 )
 
 
@@ -103,16 +103,17 @@
     loads = [
         pltpu.make_async_copy(src, dst, load_sem.at[k])
         for k, (src, dst) in enumerate((
-            (out_ref, out_in), (qkv_ref, qkv_in), (hidden_ref, hidden_in), (gain_ref, gain_in), (bias_hbm, bias_in),
+            (qkv_ref, qkv_in), (out_ref, out_in), (hidden_ref, hidden_in), (gain_ref, gain_in), (bias_hbm, bias_in),
             (len_ref, len_smem), (pos_ref, pos_smem),
         ))
     ]
-    for copy in loads:
+    for copy in loads + caches:
         copy.start()
 
     def stage(source, first, count):
-        for k in range(count):
-            tiles_ref[first + k] = source[:, k * HD : (k + 1) * HD].reshape(GROUPS, 4, HD)
+        start = first % 24
+        for k in range(start, start + count):
+            tiles_ref[first + k - start] = source[:, k * HD : (k + 1) * HD].reshape(GROUPS, 4, HD)
 
     def select_rows():
         wide = hidden_in[...].astype(F32)
@@ -175,30 +176,31 @@
         for k in range(count):
             w_ref[to + k, seq, tp, roll] = tiles_ref[first + k]
 
+    def trade_start(kind):
+        traded(kind, 0, 1).start()
+        for dy, dc in TP_STEPS:
+            if dy != 0:
+                traded(kind, dy, dc).start()
+
     loads[0].wait()
-    stage(out_in, 24, 16)
-    keep_own(0)
-    loads[1].wait()
-    stage(qkv_in, 0, 24)
+    stage(qkv_in, 0, 16)
     keep_own(1)
+    pl.semaphore_wait(barrier, len(partners))
+    trade_start(1)
+    for dx in (1, 2, 3):
+        pl.semaphore_signal(line_sem, inc=1, device_id=device(*plane_peer(dx, 0)), device_id_type=MESH)
+    stage(qkv_in, 16, 8)
     keep_own(2)
+    trade_start(2)
     for k in range(2, 7):
         loads[k].wait()
     select_rows()
-    pl.semaphore_wait(barrier, len(partners))
-    for dx in (1, 2, 3):
-        pl.semaphore_signal(line_sem, inc=1, device_id=device(*plane_peer(dx, 0)), device_id_type=MESH)
-
-    for kind in (1, 2, 0):
-        traded(kind, 0, 1).start()
     across = remote(normed_ref.at[1], other, other_sem.at[0], other_sem.at[1], plane_peer(2, 0))
     across.start()
-    for kind in (1, 2, 0):
-        for dy, dc in TP_STEPS:
-            if dy != 0:
-                traded(kind, dy, dc).start()
-    for copy in caches:
-        copy.start()
+    loads[1].wait()
+    stage(out_in, 24, 16)
+    keep_own(0)
+    trade_start(0)
     tables()
     bias_ref[...] = bias_in[...].astype(F32)
 
@@ -376,6 +378,8 @@
                     before = s_buf[rows, cols] if r > 0 else jnp.full((16, BLOCK), lowest, F32)
                     s_buf[rows, cols] = jnp.where(valid, made * HD ** (-0.5), before)
 
+    left = lax.broadcasted_iota(jnp.int32, (8, HD), 1) < HD // 2
+
     def values():
         for g in range(KVH):
             s = s_buf[16 * g : 16 * g + 16]
@@ -385,8 +389,7 @@
             low = jnp.sum(w, axis=1, keepdims=True)
             for k in range(2):
                 rows = slice(8 * k, 8 * k + 8)
-                ob[2 * g + k, 0] = jnp.broadcast_to(top[rows], (8, HD))
-                ob[2 * g + k, 1] = jnp.broadcast_to(low[rows], (8, HD))
+                ob[2 * g + k, 0] = jnp.where(left, top[rows], low[rows])
         owner = lax.broadcasted_iota(jnp.int32, (16, HERE), 0) % 4
         for r in range(4):
             caches[4 + r].wait()
@@ -396,25 +399,28 @@
             for r in range(4):
                 mine = jnp.where(owner == r, w, 0.0).astype(BF16)
                 total += jnp.dot(mine, vbuf[r, :, g * HD : (g + 1) * HD], preferred_element_type=F32)
-            ob[2 * g, 2] = total[0:8]
-            ob[2 * g + 1, 2] = total[8:16]
+            ob[2 * g, 1] = total[0:8]
+            ob[2 * g + 1, 1] = total[8:16]
         r5[tp] = ob[tp]
         tp_send(2, lambda t: ob.at[t], r5.at[tp], recv5)
 
     def combined(buffer):
-        top = buffer[0, 0]
+        tiles = [(buffer[k, 0], pltpu.roll(buffer[k, 0], 64, 1)) for k in range(8)]
+        tops = [jnp.where(left, one, two) for one, two in tiles]
+        top = tops[0]
         for k in range(1, 8):
-            top = jnp.maximum(top, buffer[k, 0])
+            top = jnp.maximum(top, tops[k])
         low, out = jnp.zeros_like(top), jnp.zeros_like(top)
         for k in range(8):
-            factor = jnp.exp(buffer[k, 0] - top)
-            low += buffer[k, 1] * factor
-            out += buffer[k, 2] * factor
+            factor = jnp.exp(tops[k] - top)
+            low += jnp.where(left, tiles[k][1], tiles[k][0]) * factor
+            out += buffer[k, 1] * factor
         return top, low, out
 
     def over_tp():
         tp_wait(2, r5, recv5)
-        for k, value in enumerate(combined(r5)):
+        top, low, out = combined(r5)
+        for k, value in enumerate((jnp.where(left, top, low), out)):
             c6[k] = value
             r6[seq, k] = value
         for dl in range(2):
@@ -569,10 +575,10 @@
             pltpu.VMEM((64, HD), F32),
             pltpu.VMEM((64, HERE), F32),
             pltpu.VMEM((64, HERE), BF16),
-            pltpu.VMEM((8, 3, 8, HD), F32),
-            pltpu.VMEM((8, 3, 8, HD), F32),
-            pltpu.VMEM((3, 8, HD), F32),
-            pltpu.VMEM((8, 3, 8, HD), F32),
+            pltpu.VMEM((8, 2, 8, HD), F32),
+            pltpu.VMEM((8, 2, 8, HD), F32),
+            pltpu.VMEM((2, 8, HD), F32),
+            pltpu.VMEM((8, 2, 8, HD), F32),
             pltpu.VMEM((8, 4, 512), F32),
             pltpu.VMEM((8, 4, 512), F32),
             pltpu.SemaphoreType.REGULAR, dma((7,)), dma((2, 4)), dma((3,)), dma((3, 8)), dma((3,)), dma((3, 40)), dma((2,)), dma((2,)),
@@ -584,7 +590,7 @@
     )(hidden, gain, bias, qkv_rows, out_rows, lengths, positions, keys, values)
 
 
-def place_kernel(w_ref, fresh_ref, final_ref, attended_ref, fresh_out, qkv_ref, out_ref, sems):
+def place_kernel(w_ref, fresh_ref, final_ref, attended_out, fresh_out, qkv_ref, out_ref, attended_ref, sems, small):
     copies = []
     for k in range(6):
         target = out_ref.at[:, k * HD : (k + 1) * HD] if k < 2 else qkv_ref.at[:, (k - 2) * HD : (k - 1) * HD]
@@ -593,9 +599,12 @@
             copies.append(pltpu.make_async_copy(w_ref.at[k, rows], target.at[rows], sems.at[k, part]))
     for copy in copies:
         copy.start()
-    fresh_out[...] = fresh_ref[...]
+    copies.append(pltpu.make_async_copy(fresh_ref, fresh_out, small.at[0]))
+    copies[-1].start()
     for o in range(8):
         attended_ref[:, o * 448 : (o + 1) * 448] = final_ref[o, :, 0:448]
+    copies.append(pltpu.make_async_copy(attended_ref, attended_out, small.at[1]))
+    copies[-1].start()
     for copy in copies:
         copy.wait()
 
@@ -612,8 +621,10 @@
             jax.ShapeDtypeStruct((3584, 256), BF16),
         ),
         in_specs=[vmem, vmem, vmem],
-        out_specs=(vmem, vmem, hbm, hbm),
-        scratch_shapes=[pltpu.SemaphoreType.DMA((6, PLACE))],
+        out_specs=(hbm, hbm, hbm, hbm),
+        scratch_shapes=[
+            pltpu.VMEM((4, 3584), BF16), pltpu.SemaphoreType.DMA((6, PLACE)), pltpu.SemaphoreType.DMA((2,)),
+        ],
         compiler_params=pltpu.CompilerParams(vmem_limit_bytes=8 * 2**20),
     )(w, fresh, final)
 

time: 49.8 us -> 48.8 us (0.980)
  Pallas kernels: 49.1 us -> 48 us
    pallas_call x1, Pallas kernels: 3.22 us -> 2.64 us  [place(): pl.pallas_call(place_kernel, name='place', out_shape=(jax.ShapeDtypeStruc...]
where the time goes in v5:
time: 48.8 us; the launch traced here: 48.7 us
  Pallas kernels  48 us (98%)
  between operations  0.64 us (1%)
    pallas_call x1, Pallas kernels, layer(): pl.pallas_call(layer_kernel, name='layer', out_shape=(jax.ShapeDtypeStruc...  45.4 us
    pallas_call x1, Pallas kernels, place(): pl.pallas_call(place_kernel, name='place', out_shape=(jax.ShapeDtypeStruc...  2.64 us

profile of v5, /device:TPU:1, one launch (start us, length us, event | category | flops | bytes accessed | tf_op | source)
XLA Modules:
  0.0 48.7 jit_solution(712946398539458852)
XLA Ops:
  0.6 45.4 %layer.1 = (bf16[6,8,8,2,7,4,128]{6,5,4,3,2,1,0:T(4,128)(2,1)S(1)}, bf16[4,1024]{1,0:T(4,128)(2,1)S(1)}, bf16[8,4,512]{2,1,0:T(4,128)(2,1)S(1)}) custom-call(bf16[4,3584]{1,0:T(4,128)(2,1)} %hidden_ref.1, bf16[3584]{0:T(1024)(128)(2,1)} %gain_ref.1, bf16[24,128]{1,0:T(8,128)(2,1)} %bitcast.4, bf16[28,3072]{1,0:T(8,128)(2,1)} %qkv_ref.1, ...), custom_call_target="tpu_custom_call" | custom-call | tf_op jit(solution)/shard_map/layer/pallas_call | solution.py:542
  46.0 2.6 %place.1 = (bf16[4,3584]{1,0:T(4,128)(2,1)}, bf16[4,1024]{1,0:T(4,128)(2,1)}, bf16[3584,512]{1,0:T(8,128)(2,1)}, bf16[3584,256]{1,0:T(8,128)(2,1)}) custom-call(bf16[6,3584,128]{2,1,0:T(8,128)(2,1)S(1)} %bitcast.3, bf16[4,1024]{1,0:T(4,128)(2,1)S(1)} %get-tuple-element.8.fresh_ref, bf16[8,4,512]{2,1,0:T(4,128)(2,1)S(1)} %get-tuple-element.9.final_ref), custom_call_target="tpu_custom_call" | custom-call | tf_op jit(solution)/shard_map/place/pallas_call | solution.py:614

commit v6 on v5

--- a/solution.py
+++ b/solution.py
@@ -43,7 +43,7 @@
 
 
 ORDER = (0, -1, 1, 2)
-TP_STEPS = tuple((dy, dc) for dy in (0, 3, 1, 2) for dc in (0, 1))
+TP_STEPS = tuple((dy, dc) for dy in (0, 2, 3, 1) for dc in (0, 1))
 PLANE_STEPS = tuple((dx, dz) for dx in (2, 1, 3, 0) for dz in (2, 1, 3, 0))
 
 

time: 48.8 us -> 48.6 us (level)
  no operation moved by 1% of the time
where the time goes in v6:
time: 48.6 us; the launch traced here: 48.5 us
  Pallas kernels  47.9 us (99%)
  between operations  0.64 us (1%)
    pallas_call x1, Pallas kernels, layer(): pl.pallas_call(layer_kernel, name='layer', out_shape=(jax.ShapeDtypeStruc...  45.2 us
    pallas_call x1, Pallas kernels, place(): pl.pallas_call(place_kernel, name='place', out_shape=(jax.ShapeDtypeStruc...  2.64 us

profile of v6, /device:TPU:1, one launch (start us, length us, event | category | flops | bytes accessed | tf_op | source)
XLA Modules:
  0.0 48.5 jit_solution(8123922455761905531)
XLA Ops:
  0.6 45.2 %layer.1 = (bf16[6,8,8,2,7,4,128]{6,5,4,3,2,1,0:T(4,128)(2,1)S(1)}, bf16[4,1024]{1,0:T(4,128)(2,1)S(1)}, bf16[8,4,512]{2,1,0:T(4,128)(2,1)S(1)}) custom-call(bf16[4,3584]{1,0:T(4,128)(2,1)} %hidden_ref.1, bf16[3584]{0:T(1024)(128)(2,1)} %gain_ref.1, bf16[24,128]{1,0:T(8,128)(2,1)} %bitcast.4, bf16[28,3072]{1,0:T(8,128)(2,1)} %qkv_ref.1, ...), custom_call_target="tpu_custom_call" | custom-call | tf_op jit(solution)/shard_map/layer/pallas_call | solution.py:542
  45.9 2.6 %place.1 = (bf16[4,3584]{1,0:T(4,128)(2,1)}, bf16[4,1024]{1,0:T(4,128)(2,1)}, bf16[3584,512]{1,0:T(8,128)(2,1)}, bf16[3584,256]{1,0:T(8,128)(2,1)}) custom-call(bf16[6,3584,128]{2,1,0:T(8,128)(2,1)S(1)} %bitcast.3, bf16[4,1024]{1,0:T(4,128)(2,1)S(1)} %get-tuple-element.8.fresh_ref, bf16[8,4,512]{2,1,0:T(4,128)(2,1)S(1)} %get-tuple-element.9.final_ref), custom_call_target="tpu_custom_call" | custom-call | tf_op jit(solution)/shard_map/place/pallas_call | solution.py:614
